TPU v7x, 768 devices: a whole 4x8x12 slice. The times are simulated.
768 devices in a mesh: dp: 96 (over y, x, z_hi), pipe: 8 (over z_lo, core).
Axes of the slice: x: 4, y: 8, z: 12 (z_hi: 3, z_lo: 4; z = z_hi * 4 + z_lo), core: 2. Of those that a mesh axis runs over, the one named last changes fastest.
Arguments:
- embed_grad: bfloat16 [6144, 4608], P('dp', 'pipe'), may hold values from -0.35 to 0.35
- ids: int32 [6144], P('dp'), may hold values from 0 to 135167
Outputs:
- table_grad: float32 [135168, 4608], P('dp', 'pipe')
All inputs are finite; a program needn't handle non-finite values.
Results may differ from a plain program's by a relative error of at most 0.00035.
Values may be sent and summed in bfloat16 or wider, within the bound.
No kernel may reach another device: no remote copies, remote signals or barrier semaphores. Data moves between devices by JAX's collectives and lax.ppermute only.
A program may use at most 64 MiB of HBM per device.

v0:
```python
import math

import jax
import jax.numpy as jnp
from jax import lax
from jax.sharding import Mesh
from jax.sharding import PartitionSpec as P

D = 4608
VOC_DEV = 1408
DP = ("dp_0", "dp_1", "dp_2")
DP_PIPE = ("dp_0", "dp_1", "dp_2", "pipe_0", "pipe_1")
PIPE = ("pipe_0", "pipe_1")


def gathered_by_axis(value, axes, dim):
    if not axes:
        return value
    nearer = lax.all_gather(value, axes[-1], axis=dim, tiled=True)
    return gathered_by_axis(nearer, axes[:-1], dim)


def one_axis_at_a_time(value, axes):
    for axis in axes:
        value = lax.psum(value, axis)
    return value


def segment_rows(cotangent, token_ids, offset):
    local = token_ids - offset
    inside = (local >= 0) & (local < VOC_DEV)
    segment = jnp.where(inside, local, VOC_DEV).astype(jnp.int32)
    summed = jax.ops.segment_sum(cotangent.astype(jnp.float32), segment, VOC_DEV + 1)
    return summed[:VOC_DEV]


def per_device(embed_grad, ids):
    offset = lax.axis_index(DP) * VOC_DEV
    summed = segment_rows(
        gathered_by_axis(embed_grad, ("dp_1", "dp_0", "dp_2"), 0),
        gathered_by_axis(ids, ("dp_1", "dp_0", "dp_2"), 0),
        offset,
    )
    grad_rows = summed * math.sqrt(D)
    total = one_axis_at_a_time(jnp.sum(grad_rows * grad_rows), DP_PIPE)
    grad_norm = jnp.sqrt(total + 1e-06)
    tokens_all = embed_grad.shape[0] * lax.axis_size(DP)
    factor = jnp.minimum(1.0, 0.2 * math.sqrt(tokens_all * D) / grad_norm)
    return grad_rows * factor


def solution(mesh):
    torus = Mesh(mesh.devices.reshape(8, 4, 3, 4, 2), ("dp_0", "dp_1", "dp_2", "pipe_0", "pipe_1"))
    return jax.shard_map(
        per_device,
        mesh=torus,
        in_specs=(P(DP, PIPE), P(DP)),
        out_specs=P(DP, PIPE),
        check_vma=False,
    )
```

profile of v0, /device:TPU:1, one launch (start us, length us, event | category | flops | bytes accessed | tf_op | source)
XLA Modules:
  0.0 287.2 jit_solution(13370928794117497934)
XLA Ops:
  6.5 0.0 all-gather.4.cloned.1.call-start
  6.5 24.5 %all_gather.21 = bf16[192,576]{1,0:T(8,128)(2,1)} all-gather(bf16[64,576]{1,0:T(8,128)(2,1)} %param.2), channel_id=1, replica_groups=mesh['dp_0'=8,'dp_1'=4,'dp_2'=3,'pipe_0'=4,'pipe_1'=2] {'dp_2'}, dimensions={0}, use_global_device_ids=true | all-gather | bytes 294912 | tf_op jit(solution)/shard_map/all_gather | solution.py:19
  31.1 0.0 all-gather.4.cloned.1.call-update
  31.1 0.0 all-gather.6.cloned.1.call-start
  31.1 42.9 %all-gather.4.cloned.1.call-done = bf16[1536,576]{1,0:T(8,128)(2,1)} async-done(((bf16[192,576]{1,0:T(8,128)(2,1)}), bf16[1536,576]{1,0:T(8,128)(2,1)}) %all-gather.4.cloned.1.call-update) | async-done | bytes 1769488 | tf_op jit(solution)/shard_map/all_gather | solution.py:19
  74.0 0.0 all-gather.6.cloned.1.call-update
  74.1 1.3 dynamic-slice.1
  75.4 1.3 dynamic-slice
  77.9 0.9 dynamic-update-slice
  78.7 11.5 %all-reduce = s32[192]{0:T(256)S(1)} all-reduce(s32[192]{0:T(256)S(1)} %dynamic-update-slice), channel_id=1, replica_groups=mesh['dp_0'=8,'dp_1'=4,'dp_2'=3,'pipe_0'=4,'pipe_1'=2] {'dp_2'}, use_global_device_ids=true, to_apply=%add | all-reduce | flops 192 | bytes 1536
  90.3 0.3 dynamic-update-slice.1
  90.5 9.4 %all-reduce.1 = s32[1536]{0:T(1024)S(1)} all-reduce(s32[1536]{0:T(1024)S(1)} %dynamic-update-slice.1), channel_id=1, replica_groups=mesh['dp_0'=8,'dp_1'=4,'dp_2'=3,'pipe_0'=4,'pipe_1'=2] {'dp_0'}, use_global_device_ids=true, to_apply=%add.1 | all-reduce | flops 1536 | bytes 12288
  99.9 10.9 %all-gather = s32[4,1,1536]{2,1,0:T(1,128)S(1)} all-gather(s32[1,1,1536]{2,1,0:T(1,128)S(1)} %reshape.15), channel_id=1, replica_groups=mesh['dp_0'=8,'dp_1'=4,'dp_2'=3,'pipe_0'=4,'pipe_1'=2] {'dp_1'}, dimensions={0}, use_global_device_ids=true | all-gather | bytes 30720 | tf_op jit(solution)/shard_map/all_gather | solution.py:19
  110.8 55.5 %all-gather.6.cloned.1.call-done = bf16[6144,576]{1,0:T(8,128)(2,1)} async-done(((bf16[1536,576]{1,0:T(8,128)(2,1)}), bf16[6144,576]{1,0:T(8,128)(2,1)}) %all-gather.6.cloned.1.call-update) | async-done | bytes 7077904 | tf_op jit(solution)/shard_map/all_gather | solution.py:19
  166.4 46.1 %scatter_custom_fusion = f32[1409,576]{1,0:T(8,128)} fusion(s32[6144]{0:T(1024)S(1)} %and_select_fusion, bf16[6144,576]{1,0:T(8,128)(2,1)} %all-gather.6.cloned.1.call-done, f32[]{:T(128)} %constant.13.clone.1), kind=kCustom, calls=%fused_computation.1 | custom fusion | flops 7077888 | bytes 10324228 | tf_op jit(solution)/shard_map/scatter-add | solution.py:33
  212.5 4.0 %slice.4 = f32[1408,576]{1,0:T(8,128)} slice(f32[1409,576]{1,0:T(8,128)} %scatter_custom_fusion), slice={[0:1408], [0:576]} | slice | bytes 6488064 | tf_op jit(solution)/shard_map/slice | solution.py:34
  216.5 3.6 %copy.7 = f32[1408,576]{0,1:T(8,128)S(1)} copy(f32[1408,576]{1,0:T(8,128)} %slice.4) | data formatting | bytes 6488064
  220.1 1.4 multiply_reduce_fusion
  221.6 14.3 %psum.35 = f32[]{:T(128)} all-reduce(f32[]{:T(128)} %multiply_reduce_fusion), channel_id=1, replica_groups=mesh['dp_0'=8,'dp_1'=4,'dp_2'=3,'pipe_0'=4,'pipe_1'=2] {'dp_0'}, use_global_device_ids=true, to_apply=%region_2.3 | all-reduce | flops 1 | bytes 8 | tf_op jit(solution)/shard_map/psum | solution.py:25
  235.8 7.6 %psum.36 = f32[]{:T(128)} all-reduce(f32[]{:T(128)} %psum.35), channel_id=1, replica_groups=mesh['dp_0'=8,'dp_1'=4,'dp_2'=3,'pipe_0'=4,'pipe_1'=2] {'dp_1'}, use_global_device_ids=true, to_apply=%region_3.4 | all-reduce | flops 1 | bytes 8 | tf_op jit(solution)/shard_map/psum | solution.py:25
  243.4 11.9 %psum.37 = f32[]{:T(128)} all-reduce(f32[]{:T(128)} %psum.36), channel_id=1, replica_groups=mesh['dp_0'=8,'dp_1'=4,'dp_2'=3,'pipe_0'=4,'pipe_1'=2] {'dp_2'}, use_global_device_ids=true, to_apply=%region_4.5 | all-reduce | flops 1 | bytes 8 | tf_op jit(solution)/shard_map/psum | solution.py:25
  255.3 10.2 %psum.38 = f32[]{:T(128)} all-reduce(f32[]{:T(128)} %psum.37), channel_id=1, replica_groups=mesh['dp_0'=8,'dp_1'=4,'dp_2'=3,'pipe_0'=4,'pipe_1'=2] {'pipe_0'}, use_global_device_ids=true, to_apply=%region_5.6 | all-reduce | flops 1 | bytes 8 | tf_op jit(solution)/shard_map/psum | solution.py:25
  265.5 12.2 %psum.39 = f32[]{:T(128)} all-reduce(f32[]{:T(128)} %psum.38), channel_id=1, replica_groups=mesh['dp_0'=8,'dp_1'=4,'dp_2'=3,'pipe_0'=4,'pipe_1'=2] {'pipe_1'}, use_global_device_ids=true, to_apply=%region_6.7 | all-reduce | flops 1 | bytes 8 | tf_op jit(solution)/shard_map/psum | solution.py:25
  278.4 1.9 broadcast_multiply_fusion
  (5 shorter events, 0.0 us)
Async XLA Ops:
  6.5 67.5 %all-gather.4.cloned.1.call-start = ((), (), s32[]{:S(2)}) async-start(), calls=%async_computation | async-start | bytes 2211840 | tf_op jit(solution)/shard_map/all_gather | solution.py:19
  31.1 135.3 %all-gather.6.cloned.1.call-start = ((), (), s32[]{:S(2)}) async-start(), calls=%async_computation.1 | async-start | bytes 9830400 | tf_op jit(solution)/shard_map/all_gather | solution.py:19
Sparse Core Ops, SparseCore 0:
  31.2 42.7 all-gather.3
  76.4 89.8 all-gather.5
where the time goes:
time: 288 us; the launch traced here: 287 us
  blocking collectives  112 us (39%)
  waiting for transfers between devices  98.5 us (34%)
  other arithmetic  49.5 us (17%)
  between operations  15.4 us (5%)
  local copies, waits for them, and re-layouts  11.3 us (4%)
    all_gather x2, waiting for transfers between devices, gathered_by_axis(): nearer = lax.all_gather(value, axes[-1], axis=dim, tiled=True)  98.4 us
    psum x5, blocking collectives, one_axis_at_a_time(): value = lax.psum(value, axis)  56.2 us
    scatter-add x1, other arithmetic, segment_rows(): jax.ops.segment_sum(cotangent.astype(jnp.float32), segment, VOC_DEV + 1)  46.1 us
    all_gather x2, blocking collectives, gathered_by_axis(): nearer = lax.all_gather(value, axes[-1], axis=dim, tiled=True)  35.4 us
    unnamed x2, blocking collectives  20.9 us
    unnamed x8, local copies, waits for them, and re-layouts  7.3 us
  transfers between devices with their start and end apart: 2, of which 2 were waited for; matrix products, arithmetic and copies ran while one was open for 1% of the time, Pallas kernels for 0%

commit v1 on v0

v1 whole, which is shorter than its diff:
```python
import functools
import math

import jax
import jax.numpy as jnp
from jax import lax
from jax.experimental import pallas as pl
from jax.experimental.pallas import tpu as pltpu
from jax.sharding import Mesh
from jax.sharding import PartitionSpec as P

D = 4608
VOC_DEV = 1408
WIDE = 640
TAIL = 512
AUX = 64
Y, X, ZH, ZL, CORE = AXES = ("dp_0", "dp_1", "dp_2", "pipe_0", "pipe_1")
DP = AXES[:3]
PIPE = AXES[3:]
F32 = jnp.float32
BF16 = jnp.bfloat16

FIRST = (ZH,)
FIRST_CAP = 48
SECOND = (Y, X)
SECOND_CAP = 16
NORM_1 = (Y, X, CORE)
NORM_2 = (ZH, ZL)


def axis_size(axes):
    return math.prod({Y: 8, X: 4, ZH: 3, ZL: 4, CORE: 2}[a] for a in axes)


def floor_div(value, by):
    return jnp.floor((value + 0.5) * (1.0 / by))


def place(code, axes):
    y = floor_div(code - 1.0, 12 * VOC_DEV)
    rest = code - 1.0 - y * (12 * VOC_DEV)
    x = floor_div(rest, 3 * VOC_DEV)
    zh = floor_div(rest - x * (3 * VOC_DEV), VOC_DEV)
    index = 0.0
    for axis in axes:
        index = index * axis_size((axis,)) + {Y: y, X: x, ZH: zh}[axis]
    return index


def square_iota(n):
    return (lax.broadcasted_iota(jnp.int32, (n, n), 0), lax.broadcasted_iota(jnp.int32, (n, n), 1))


def column_to_row(column):
    i, j = square_iota(column.shape[0])
    return jnp.sum(jnp.where(i == j, column, 0.0), axis=0, keepdims=True)


def row_to_column(row):
    i, j = square_iota(row.shape[1])
    return jnp.sum(jnp.where(i == j, row, 0.0), axis=1, keepdims=True)


def decode(tail):
    lane = lax.broadcasted_iota(jnp.int32, (1, 128), 1)
    weight = jnp.where(lane == AUX, 1024.0, jnp.where(lane == AUX + 1, 8.0, jnp.where(lane == AUX + 2, 1.0, 0.0)))
    return jnp.sum(tail.astype(F32) * weight, axis=1, keepdims=True)


def encode(code):
    high = jnp.floor(code * (1.0 / 1024))
    rest = code - high * 1024.0
    middle = jnp.floor(rest * (1.0 / 8))
    low = rest - middle * 8.0
    lane = lax.broadcasted_iota(jnp.int32, (1, 128), 1)
    return jnp.where(lane == AUX, high, jnp.where(lane == AUX + 1, middle, jnp.where(lane == AUX + 2, low, 0.0)))


def pack(code_row, code_col, axes, cap):
    n = code_row.shape[1]
    i, j = square_iota(n)
    real_row = code_row > 0.5
    real_col = code_col > 0.5
    to_row = jnp.where(real_row, place(code_row, axes), -1.0)
    to_col = jnp.where(real_col, place(code_col, axes), -1.0)
    same = jnp.where((code_col == code_row) & real_row, 1.0, 0.0)
    above = jnp.where(i < j, same, 0.0)
    below = jnp.where(j < i, same, 0.0)
    count_row = jnp.sum(same, axis=0, keepdims=True)
    lead_row = (jnp.sum(above, axis=0, keepdims=True) == 0.0) & real_row
    lead_col = (jnp.sum(below, axis=1, keepdims=True) == 0.0) & real_col
    width_row = jnp.where(lead_row, jnp.minimum(count_row, 2.0), 0.0)
    before = jnp.sum(jnp.where((to_col == to_row) & (j < i), width_row, 0.0), axis=1, keepdims=True)
    before = jnp.where(lead_col, before, 0.0)
    slot_in = jnp.sum(same * before, axis=0, keepdims=True)
    over = jnp.max(jnp.where(real_row & (slot_in + jnp.minimum(count_row, 2.0) > cap), 1.0, 0.0), axis=1, keepdims=True)
    base = jnp.where(real_row, to_row * cap + slot_in, -2.0)
    return base, count_row, lead_row, over


def fill(out_ref, base, count_row, lead_row, code_row, head, tail, slots):
    n = base.shape[1]
    slot = lax.broadcasted_iota(jnp.int32, (slots, n), 0).astype(F32)
    first = slot == base
    second = (slot == base + 1.0) & (count_row > 1.5)
    take = jnp.where(first | second, 1.0, 0.0)
    code = jnp.sum(jnp.where(lead_row, take * code_row, 0.0), axis=1, keepdims=True)
    is_second = jnp.max(jnp.where(second, 1.0, 0.0), axis=1, keepdims=True) > 0.5
    take = take.astype(BF16)

    def split(rows):
        total = jnp.dot(take, rows, preferred_element_type=F32)
        kept = total.astype(BF16).astype(F32)
        return jnp.where(is_second, total - kept, kept)

    out_ref[:, :TAIL] = split(head).astype(BF16)
    lane = lax.broadcasted_iota(jnp.int32, (1, 128), 1)
    out_ref[:, TAIL:] = jnp.where(lane < AUX, split(tail), encode(code)).astype(BF16)


def first_kernel(grad_ref, ids_ref, out_ref, over_ref):
    code_row = ids_ref[...].astype(F32) + 1.0
    code_col = row_to_column(code_row)
    slots = out_ref.shape[0]
    base, count, lead, over = pack(code_row, code_col, FIRST, FIRST_CAP)
    tail = grad_ref[:, TAIL:]
    tail = jnp.concatenate([tail, jnp.zeros_like(tail)], axis=1)
    fill(out_ref, base, count, lead, code_row, grad_ref[:, :TAIL], tail, slots)
    over_ref[...] = jnp.broadcast_to(over, over_ref.shape)


def second_kernel(rows_ref, over_in_ref, out_ref, over_ref):
    tail = rows_ref[:, TAIL:]
    code_col = decode(tail)
    code_row = column_to_row(code_col)
    base, count, lead, over = pack(code_row, code_col, SECOND, SECOND_CAP)
    fill(out_ref, base, count, lead, code_row, rows_ref[:, :TAIL], tail, out_ref.shape[0])
    over_ref[...] = jnp.broadcast_to(over, over_ref.shape) + over_in_ref[...]


def features(rows_ref):
    lane = lax.broadcasted_iota(jnp.int32, (1, 128), 1)
    tail = rows_ref[:, TAIL:]
    return rows_ref[:, :TAIL], jnp.where(lane < AUX, tail.astype(F32), 0.0).astype(BF16)


def norm_kernel(rows_ref, over_ref, part_ref):
    code_col = decode(rows_ref[:, TAIL:])
    code_row = column_to_row(code_col)
    head, tail = features(rows_ref)
    nt = (((1,), (1,)), ((), ()))
    gram = lax.dot_general(head, head, nt, preferred_element_type=F32)
    gram = gram + lax.dot_general(tail, tail, nt, preferred_element_type=F32)
    gram = jnp.where((code_col == code_row) & (code_row > 0.5), gram, 0.0)
    squares = jnp.sum(jnp.sum(gram, axis=0, keepdims=True), axis=1, keepdims=True)
    lane = lax.broadcasted_iota(jnp.int32, (1, 128), 1)
    part = jnp.where(lane == 0, squares, jnp.where(lane == 1, over_ref[:1, :], 0.0))
    part_ref[...] = jnp.broadcast_to(part[:, None, :], part_ref.shape)


def clip_factor(total, tokens):
    grad_norm = jnp.sqrt(total * float(D) + 1e-06)
    return jnp.minimum(1.0, 0.2 * math.sqrt(tokens * D) / grad_norm)


BLOCK = 384


def write_kernel(rows_ref, parts_ref, out_ref, turned_ref, *, tokens):
    @pl.when(pl.program_id(0) == 0)
    def _():
        turned_ref[...] = rows_ref[...].T

    lane = lax.broadcasted_iota(jnp.int32, (1, 128), 1)
    total = jnp.sum(parts_ref[...], axis=0)
    total = jnp.sum(jnp.where(lane == 0, total, 0.0), axis=1, keepdims=True)
    scale = clip_factor(total, tokens) * math.sqrt(D)
    code = decode(rows_ref[:, TAIL:])
    local = code - 1.0
    local = jnp.where(code > 0.5, local - VOC_DEV * floor_div(local, VOC_DEV), -1.0)
    here = lax.broadcasted_iota(jnp.int32, (local.shape[0], BLOCK), 1) + pl.program_id(0) * BLOCK
    pick = jnp.where(here.astype(F32) == local, 1.0, 0.0).astype(BF16)
    features = out_ref.shape[0]
    out_ref[...] = jnp.dot(turned_ref[:features, :], pick, preferred_element_type=F32) * scale


def shape(rows, cols, dtype=F32):
    return jax.ShapeDtypeStruct((rows, cols), dtype)


def around(axes, sizes, value, body, init):
    if not axes:
        return value, body(value, init)
    axis, n = axes[0], sizes[0]
    ring = [(k, (k + 1) % n) for k in range(n)]

    def step(_, carry):
        held, acc = around(axes[1:], sizes[1:], carry[0], body, carry[1])
        return jax.tree.map(lambda a: lax.ppermute(a, axis, ring), held), acc

    return lax.fori_loop(0, n, step, (value, init))


def general(embed_grad, ids):
    tokens = ids.shape[0]
    offset = lax.axis_index(DP) * VOC_DEV

    def add(held, acc):
        rows, names = held
        here = lax.broadcasted_iota(jnp.int32, (VOC_DEV, tokens), 0)
        pick = (here == (names[0] - offset)[None, :]).astype(BF16)
        return acc + jnp.dot(pick, rows, preferred_element_type=F32)

    names = jnp.broadcast_to(ids[None, :], (8, tokens))
    zeros = jnp.zeros((VOC_DEV, embed_grad.shape[1]), F32)
    _, summed = around(DP, (8, 4, 3), (embed_grad, names), add, zeros)
    total = jnp.sum(summed * summed)
    for axis in AXES:
        total = lax.psum(total, axis)
    return summed * (clip_factor(total, tokens * 96) * math.sqrt(D))


def per_device(embed_grad, ids):
    tokens = ids.shape[0]
    cols = embed_grad.shape[1]
    slots_1 = axis_size(FIRST) * FIRST_CAP
    slots_2 = axis_size(SECOND) * SECOND_CAP
    sent, over = pl.pallas_call(first_kernel, out_shape=(shape(slots_1, WIDE, BF16), shape(8, 128)), name="first")(
        embed_grad, ids.reshape(1, tokens)
    )
    held = lax.all_to_all(sent, FIRST, 0, 0, tiled=True)
    sent, over = pl.pallas_call(second_kernel, out_shape=(shape(slots_2, WIDE, BF16), shape(8, 128)), name="second")(
        held, over
    )
    held = lax.all_to_all(sent, SECOND, 0, 0, tiled=True)
    n1, n2 = axis_size(NORM_1), axis_size(NORM_2)
    part = pl.pallas_call(norm_kernel, out_shape=jax.ShapeDtypeStruct((n1, 1, 128), F32), name="squares")(held, over)
    part = lax.all_to_all(part, NORM_1, 0, 0, tiled=True)
    part = jnp.broadcast_to(jnp.sum(part, axis=0, keepdims=True), (n2, 1, 128))
    part = lax.all_to_all(part, NORM_2, 0, 0, tiled=True)
    overflow = jnp.sum(part[:, 0, 1])

    def routed():
        return pl.pallas_call(
            functools.partial(write_kernel, tokens=tokens * 96),
            grid=(pl.cdiv(VOC_DEV, BLOCK),),
            in_specs=[
                pl.BlockSpec((slots_2, WIDE), lambda b: (0, 0)),
                pl.BlockSpec((n2, 1, 128), lambda b: (0, 0, 0)),
            ],
            out_specs=pl.BlockSpec((cols, BLOCK), lambda b: (0, b)),
            out_shape=shape(cols, VOC_DEV),
            scratch_shapes=[pltpu.VMEM((WIDE, slots_2), BF16)],
            name="rows",
        )(held, part).T

    return lax.cond(overflow > 0.0, lambda: general(embed_grad, ids), routed)


def solution(mesh):
    torus = Mesh(mesh.devices.reshape(8, 4, 3, 4, 2), AXES)
    return jax.shard_map(
        per_device,
        mesh=torus,
        in_specs=(P(DP, PIPE), P(DP)),
        out_specs=P(DP, PIPE),
        check_vma=False,
    )
```

time: 288 us -> 98.5 us (0.34)
  waiting for transfers between devices: 98.5 us -> 8.87 us
  other arithmetic: 49.5 us -> 0.77 us
  blocking collectives: 112 us -> 67.3 us
  between operations: 15.4 us -> 0.68 us
  Pallas kernels: 0 us -> 10.1 us
  local copies, waits for them, and re-layouts: 11.3 us -> 1.49 us
  starting transfers between devices: 0.04 us -> 8.88 us
    all_gather x2 -> x0, waiting for transfers between devices: 98.4 us -> none  [gathered_by_axis(): nearer = lax.all_gather(value, axes[-1], axis=dim, tiled=True)]
    all_to_all x0 -> x3, blocking collectives: none -> 67.3 us  [the longest x1 26.4 us: per_device(): held = lax.all_to_all(sent, SECOND, 0, 0, tiled=True)]
    psum x5 -> x0, blocking collectives: 56.2 us -> none  [one_axis_at_a_time(): value = lax.psum(value, axis)]
    scatter-add x1 -> x0, other arithmetic: 46.1 us -> none  [segment_rows(): jax.ops.segment_sum(cotangent.astype(jnp.float32), segment, VOC_DEV + 1)]
    all_gather x2 -> x0, blocking collectives: 35.4 us -> none  [gathered_by_axis(): nearer = lax.all_gather(value, axes[-1], axis=dim, tiled=True)]
    unnamed x2 -> x0, blocking collectives: 20.9 us -> none
    pallas_call x0 -> x4, Pallas kernels: none -> 10.1 us  [the longest x1 3.74 us: routed(): pl.pallas_call(functools.partial(write_kernel, tokens=tokens * 96), grid=...]
    all_to_all x0 -> x1, starting transfers between devices: none -> 8.88 us  [per_device(): part = lax.all_to_all(part, NORM_2, 0, 0, tiled=True)]
  transfers between devices with their start and end apart: 2 -> 1, of which waited for: 2 -> 1; matrix products, arithmetic and copies ran while one was open for 1% -> 0% of each run, Pallas kernels for 0% -> 0%
where the time goes in v1:
time: 98.5 us; the launch traced here: 98 us
  blocking collectives  67.3 us (68%)
  Pallas kernels  10.1 us (10%)
  starting transfers between devices  8.88 us (9%)
  waiting for transfers between devices  8.87 us (9%)
  local copies, waits for them, and re-layouts  1.49 us (2%)
    all_to_all x1, blocking collectives, per_device(): held = lax.all_to_all(sent, SECOND, 0, 0, tiled=True)  26.4 us
    all_to_all x1, blocking collectives, per_device(): held = lax.all_to_all(sent, FIRST, 0, 0, tiled=True)  22 us
    all_to_all x1, blocking collectives, per_device(): part = lax.all_to_all(part, NORM_1, 0, 0, tiled=True)  18.9 us
    all_to_all x1, starting transfers between devices, per_device(): part = lax.all_to_all(part, NORM_2, 0, 0, tiled=True)  8.88 us
    all_to_all x1, waiting for transfers between devices, per_device(): part = lax.all_to_all(part, NORM_2, 0, 0, tiled=True)  8.87 us
    pallas_call x1, Pallas kernels, routed(): pl.pallas_call(functools.partial(write_kernel, tokens=tokens * 96), grid=...  3.74 us
    pallas_call x1, Pallas kernels, per_device(): pl.pallas_call(second_kernel, out_shape=(shape(slots_2, WIDE, BF16), shap...  2.62 us
    pallas_call x1, Pallas kernels, per_device(): pl.pallas_call(norm_kernel, out_shape=jax.ShapeDtypeStruct((n1, 1, 128),...  1.98 us
  transfers between devices with their start and end apart: 1, of which 1 were waited for; matrix products, arithmetic and copies ran while one was open for 0% of the time, Pallas kernels for 0%

profile of v1, /device:TPU:1, one launch (start us, length us, event | category | flops | bytes accessed | tf_op | source)
XLA Modules:
  0.0 98.0 jit_solution(12363479086683440987)
XLA Ops:
  0.0 0.9 copy.46.grad_ref
  0.9 0.0 copy-start
  0.9 1.7 %first.1 = (bf16[144,640]{1,0:T(8,128)(2,1)}, f32[8,128]{1,0:T(8,128)}) custom-call(bf16[64,576]{1,0:T(8,128)(2,1)S(1)} %copy.46.grad_ref, s32[1,64]{1,0:T(1,128)} %bitcast.19), custom_call_target="tpu_custom_call" | custom-call | tf_op jit(solution)/shard_map/first/pallas_call | solution.py:228
  2.6 22.0 %all_to_all.32 = bf16[3,48,640]{2,1,0:T(8,128)(2,1)} all-to-all(bf16[3,48,640]{2,1,0:T(8,128)(2,1)} %bitcast.18), channel_id=1, replica_groups=mesh['dp_0'=8,'dp_1'=4,'dp_2'=3,'pipe_0'=4,'pipe_1'=2] {'dp_2'}, dimensions={0} | all-to-all | bytes 368640 | tf_op jit(solution)/shard_map/all_to_all | solution.py:231
  24.6 2.6 %second.1 = (bf16[512,640]{1,0:T(8,128)(2,1)}, f32[8,128]{1,0:T(8,128)}) custom-call(bf16[144,640]{1,0:T(8,128)(2,1)} %bitcast.16, f32[8,128]{1,0:T(8,128)} %get-tuple-element.110.over_in_ref), custom_call_target="tpu_custom_call" | custom-call | tf_op jit(solution)/shard_map/second/pallas_call | solution.py:232
  27.2 26.4 %all_to_all.33 = bf16[32,16,640]{2,1,0:T(8,128)(2,1)S(1)} all-to-all(bf16[32,16,640]{2,1,0:T(8,128)(2,1)} %bitcast.17), channel_id=1, replica_groups=mesh['dp_0'=8,'dp_1'=4,'dp_2'=3,'pipe_0'=4,'pipe_1'=2] {'dp_0','dp_1'}, dimensions={0} | all-to-all | bytes 1310720 | tf_op jit(solution)/shard_map/all_to_all | solution.py:235
  53.6 2.0 %squares.1 = f32[64,1,128]{2,1,0:T(1,128)} custom-call(bf16[512,640]{1,0:T(8,128)(2,1)S(1)} %bitcast.13, f32[8,128]{1,0:T(8,128)} %get-tuple-element.112.over_ref), custom_call_target="tpu_custom_call" | custom-call | tf_op jit(solution)/shard_map/squares/pallas_call | solution.py:237
  55.6 18.9 %all_to_all.34 = f32[64,1,128]{2,1,0:T(1,128)S(1)} all-to-all(f32[64,1,128]{2,1,0:T(1,128)} %squares.1), channel_id=1, replica_groups=mesh['dp_0'=8,'dp_1'=4,'dp_2'=3,'pipe_0'=4,'pipe_1'=2] {'dp_0','dp_1','p..., dimensions={0} | all-to-all | bytes 65536 | tf_op jit(solution)/shard_map/all_to_all | solution.py:238
  74.5 0.1 reduce_sum.27
  74.6 0.6 broadcast_in_dim.4
  75.2 8.9 %all-to-all-start.3 = ((f32[12,1,128]{2,1,0:T(1,128)}), f32[12,1,128]{2,1,0:T(1,128)S(1)}, u32[]{:S(2)}, u32[]{:S(2)}) async-start(f32[12,1,128]{2,1,0:T(1,128)} %broadcast_in_dim.4), calls=%async_computation.3 | async-start | bytes 12288 | tf_op jit(solution)/shard_map/all_to_all | solution.py:240
  84.1 8.9 %all-to-all-done.3 = f32[12,1,128]{2,1,0:T(1,128)S(1)} async-done(((f32[12,1,128]{2,1,0:T(1,128)}), f32[12,1,128]{2,1,0:T(1,128)S(1)}, u32[]{:S(2)}, u32[]{:S(2)}) %all-to-all-start.3) | async-done | bytes 6176 | tf_op jit(solution)/shard_map/all_to_all | solution.py:240
  92.9 0.7 slice_reduce_fusion
  94.3 0.0 copy-done
  94.3 3.7 %conditional.1 = (f32[1408,576]{0,1:T(8,128)}) conditional(s32[]{:T(128)} %convert_element_type.4, (bf16[512,640]{1,0:T(8,128)(2,1)S(1)}, f32[12,1,128]{2,1,0:T(1,128)S(1)}) %tuple.72, (s32[64]{0:T(128)}, bf16[64,576]{1,0:T(8,128)(2,1)}) %tuple.70), branch_computations={%region_2.0_spmd, %region_3.0_spmd} | conditional | flops 107143248 | bytes 21200900 | solution.py:257
  94.3 3.7 %rows.1 = f32[576,1408]{1,0:T(8,128)} custom-call(bf16[512,640]{1,0:T(8,128)(2,1)S(1)} %get-tuple-element.76.rows_ref, f32[12,1,128]{2,1,0:T(1,128)S(1)} %get-tuple-element.77.parts_ref), custom_call_target="tpu_custom_call" | custom-call | tf_op jit(solution)/shard_map/cond/branch_0_fun/rows/pallas_call | solution.py:244
Async XLA Ops:
  0.9 93.4 %copy-start = (bf16[64,576]{1,0:T(8,128)(2,1)}, bf16[64,576]{1,0:T(8,128)(2,1)S(1)}, u32[]{:S(2)}) copy-start(bf16[64,576]{1,0:T(8,128)(2,1)S(1)} %copy.46.grad_ref) | copy-start | bytes 221188
  75.2 17.8 %all-to-all-start.3 = ((f32[12,1,128]{2,1,0:T(1,128)}), f32[12,1,128]{2,1,0:T(1,128)S(1)}, u32[]{:S(2)}, u32[]{:S(2)}) async-start(f32[12,1,128]{2,1,0:T(1,128)} %broadcast_in_dim.4), calls=%async_computation.3 | async-start | bytes 12288 | tf_op jit(solution)/shard_map/all_to_all | solution.py:240

commit v2 on v1

--- a/solution.py
+++ b/solution.py
@@ -20,10 +20,10 @@
 F32 = jnp.float32
 BF16 = jnp.bfloat16
 
-FIRST = (ZH,)
-FIRST_CAP = 48
-SECOND = (Y, X)
-SECOND_CAP = 16
+FIRST = (Y,)
+FIRST_CAP = 24
+SECOND = (ZH, X)
+SECOND_CAP = 24
 NORM_1 = (Y, X, CORE)
 NORM_2 = (ZH, ZL)
 
@@ -118,15 +118,18 @@
     out_ref[:, TAIL:] = jnp.where(lane < AUX, split(tail), encode(code)).astype(BF16)
 
 
-def first_kernel(grad_ref, ids_ref, out_ref, over_ref):
+def first_kernel(grad_hbm, ids_ref, out_ref, over_ref, grad_ref, sem):
+    load = pltpu.make_async_copy(grad_hbm, grad_ref, sem)
+    load.start()
     code_row = ids_ref[...].astype(F32) + 1.0
     code_col = row_to_column(code_row)
     slots = out_ref.shape[0]
     base, count, lead, over = pack(code_row, code_col, FIRST, FIRST_CAP)
+    over_ref[...] = jnp.broadcast_to(over, over_ref.shape)
+    load.wait()
     tail = grad_ref[:, TAIL:]
     tail = jnp.concatenate([tail, jnp.zeros_like(tail)], axis=1)
     fill(out_ref, base, count, lead, code_row, grad_ref[:, :TAIL], tail, slots)
-    over_ref[...] = jnp.broadcast_to(over, over_ref.shape)
 
 
 def second_kernel(rows_ref, over_in_ref, out_ref, over_ref):
@@ -163,29 +166,35 @@
     return jnp.minimum(1.0, 0.2 * math.sqrt(tokens * D) / grad_norm)
 
 
-BLOCK = 384
-
-
-def write_kernel(rows_ref, parts_ref, out_ref, turned_ref, *, tokens):
-    @pl.when(pl.program_id(0) == 0)
-    def _():
-        turned_ref[...] = rows_ref[...].T
-
+EDGES = (0, 384, 768, 1152, VOC_DEV)
+
+
+def write_kernel(rows_ref, parts_ref, out_hbm, made_ref, sems, *, tokens):
+    turned = rows_ref[...].T[: made_ref.shape[0], :]
     lane = lax.broadcasted_iota(jnp.int32, (1, 128), 1)
     total = jnp.sum(parts_ref[...], axis=0)
     total = jnp.sum(jnp.where(lane == 0, total, 0.0), axis=1, keepdims=True)
     scale = clip_factor(total, tokens) * math.sqrt(D)
     code = decode(rows_ref[:, TAIL:])
     local = code - 1.0
-    local = jnp.where(code > 0.5, local - VOC_DEV * floor_div(local, VOC_DEV), -1.0)
-    here = lax.broadcasted_iota(jnp.int32, (local.shape[0], BLOCK), 1) + pl.program_id(0) * BLOCK
-    pick = jnp.where(here.astype(F32) == local, 1.0, 0.0).astype(BF16)
-    features = out_ref.shape[0]
-    out_ref[...] = jnp.dot(turned_ref[:features, :], pick, preferred_element_type=F32) * scale
+    local = jnp.where(code > 0.5, local - VOC_DEV * floor_div(local, VOC_DEV), -1.0).astype(jnp.int32)
+    copies = []
+    for k, (low, high) in enumerate(zip(EDGES[:-1], EDGES[1:])):
+        here = lax.broadcasted_iota(jnp.int32, (local.shape[0], high - low), 1) + low
+        pick = jnp.where(here == local, 1.0, 0.0).astype(BF16)
+        made_ref[:, low:high] = jnp.dot(turned, pick, preferred_element_type=F32) * scale
+        copies.append(pltpu.make_async_copy(made_ref.at[:, low:high], out_hbm.at[:, low:high], sems.at[k]))
+        copies[-1].start()
+    for copy in copies:
+        copy.wait()
 
 
 def shape(rows, cols, dtype=F32):
     return jax.ShapeDtypeStruct((rows, cols), dtype)
+
+
+def near(dims, dtype=F32):
+    return pltpu.VMEM(dims, dtype)
 
 
 def around(axes, sizes, value, body, init):
@@ -212,8 +221,10 @@
         return acc + jnp.dot(pick, rows, preferred_element_type=F32)
 
     names = jnp.broadcast_to(ids[None, :], (8, tokens))
-    zeros = jnp.zeros((VOC_DEV, embed_grad.shape[1]), F32)
-    _, summed = around(DP, (8, 4, 3), (embed_grad, names), add, zeros)
+    cols = embed_grad.shape[1]
+    padded = jnp.pad(embed_grad, ((0, 0), (0, WIDE - cols)))
+    _, summed = around(DP, (8, 4, 3), (padded, names), add, jnp.zeros((VOC_DEV, WIDE), F32))
+    summed = summed[:, :cols]
     total = jnp.sum(summed * summed)
     for axis in AXES:
         total = lax.psum(total, axis)
@@ -225,16 +236,20 @@
     cols = embed_grad.shape[1]
     slots_1 = axis_size(FIRST) * FIRST_CAP
     slots_2 = axis_size(SECOND) * SECOND_CAP
-    sent, over = pl.pallas_call(first_kernel, out_shape=(shape(slots_1, WIDE, BF16), shape(8, 128)), name="first")(
-        embed_grad, ids.reshape(1, tokens)
-    )
+    sent, over = pl.pallas_call(
+        first_kernel,
+        in_specs=[pl.BlockSpec(memory_space=pltpu.HBM), pl.BlockSpec(memory_space=pltpu.VMEM)],
+        out_shape=(near((slots_1, WIDE), BF16), near((8, 128))),
+        scratch_shapes=[pltpu.VMEM((tokens, cols), BF16), pltpu.SemaphoreType.DMA],
+        name="first",
+    )(pltpu.with_memory_space_constraint(embed_grad, pltpu.HBM), ids.reshape(1, tokens))
     held = lax.all_to_all(sent, FIRST, 0, 0, tiled=True)
-    sent, over = pl.pallas_call(second_kernel, out_shape=(shape(slots_2, WIDE, BF16), shape(8, 128)), name="second")(
+    sent, over = pl.pallas_call(second_kernel, out_shape=(near((slots_2, WIDE), BF16), near((8, 128))), name="second")(
         held, over
     )
     held = lax.all_to_all(sent, SECOND, 0, 0, tiled=True)
     n1, n2 = axis_size(NORM_1), axis_size(NORM_2)
-    part = pl.pallas_call(norm_kernel, out_shape=jax.ShapeDtypeStruct((n1, 1, 128), F32), name="squares")(held, over)
+    part = pl.pallas_call(norm_kernel, out_shape=near((n1, 1, 128)), name="squares")(held, over)
     part = lax.all_to_all(part, NORM_1, 0, 0, tiled=True)
     part = jnp.broadcast_to(jnp.sum(part, axis=0, keepdims=True), (n2, 1, 128))
     part = lax.all_to_all(part, NORM_2, 0, 0, tiled=True)
@@ -243,14 +258,10 @@
     def routed():
         return pl.pallas_call(
             functools.partial(write_kernel, tokens=tokens * 96),
-            grid=(pl.cdiv(VOC_DEV, BLOCK),),
-            in_specs=[
-                pl.BlockSpec((slots_2, WIDE), lambda b: (0, 0)),
-                pl.BlockSpec((n2, 1, 128), lambda b: (0, 0, 0)),
-            ],
-            out_specs=pl.BlockSpec((cols, BLOCK), lambda b: (0, b)),
+            in_specs=[pl.BlockSpec(memory_space=pltpu.VMEM)] * 2,
+            out_specs=pl.BlockSpec(memory_space=pltpu.HBM),
             out_shape=shape(cols, VOC_DEV),
-            scratch_shapes=[pltpu.VMEM((WIDE, slots_2), BF16)],
+            scratch_shapes=[pltpu.VMEM((cols, VOC_DEV), F32), pltpu.SemaphoreType.DMA((len(EDGES) - 1,))],
             name="rows",
         )(held, part).T
 

time: 98.5 us -> 90 us (0.914)
  starting transfers between devices: 8.88 us -> 4.99 us
  Pallas kernels: 10.1 us -> 7.06 us
    all_to_all x1, blocking collectives: 22 us -> 16.7 us  [per_device(): held = lax.all_to_all(sent, FIRST, 0, 0, tiled=True)]
    all_to_all x1, starting transfers between devices: 8.88 us -> 4.99 us  [per_device(): part = lax.all_to_all(part, NORM_2, 0, 0, tiled=True)]
    pallas_call x4, Pallas kernels: 10.1 us -> 7.06 us  [the longest x1 2.49 us: routed(): pl.pallas_call(functools.partial(write_kernel, tokens=tokens * 96), in_sp...]
    all_to_all x1, blocking collectives: 26.4 us -> 29.2 us  [per_device(): held = lax.all_to_all(sent, SECOND, 0, 0, tiled=True)]
    all_to_all x1, blocking collectives: 18.9 us -> 20.7 us  [per_device(): part = lax.all_to_all(part, NORM_1, 0, 0, tiled=True)]
where the time goes in v2:
time: 90 us; the launch traced here: 89.6 us
  blocking collectives  66.6 us (74%)
  waiting for transfers between devices  8.87 us (10%)
  Pallas kernels  7.06 us (8%)
  starting transfers between devices  4.99 us (6%)
    all_to_all x1, blocking collectives, per_device(): held = lax.all_to_all(sent, SECOND, 0, 0, tiled=True)  29.2 us
    all_to_all x1, blocking collectives, per_device(): part = lax.all_to_all(part, NORM_1, 0, 0, tiled=True)  20.7 us
    all_to_all x1, blocking collectives, per_device(): held = lax.all_to_all(sent, FIRST, 0, 0, tiled=True)  16.7 us
    all_to_all x1, waiting for transfers between devices, per_device(): part = lax.all_to_all(part, NORM_2, 0, 0, tiled=True)  8.87 us
    all_to_all x1, starting transfers between devices, per_device(): part = lax.all_to_all(part, NORM_2, 0, 0, tiled=True)  4.99 us
    pallas_call x1, Pallas kernels, routed(): pl.pallas_call(functools.partial(write_kernel, tokens=tokens * 96), in_sp...  2.49 us
  transfers between devices with their start and end apart: 1, of which 1 were waited for; matrix products, arithmetic and copies ran while one was open for 0% of the time, Pallas kernels for 0%

profile of v2, /device:TPU:1, one launch (start us, length us, event | category | flops | bytes accessed | tf_op | source)
XLA Modules:
  0.0 89.6 jit_solution(1604765650300633235)
XLA Ops:
  0.0 1.8 %first.1 = (bf16[192,640]{1,0:T(8,128)(2,1)S(1)}, f32[8,128]{1,0:T(8,128)S(1)}) custom-call(bf16[64,576]{1,0:T(8,128)(2,1)} %grad_hbm.1, s32[1,64]{1,0:T(1,128)} %bitcast.19), custom_call_target="tpu_custom_call" | custom-call | tf_op jit(solution)/shard_map/first/pallas_call | solution.py:239
  1.8 0.0 copy-start
  1.8 16.7 %all_to_all.32 = bf16[8,24,640]{2,1,0:T(8,128)(2,1)} all-to-all(bf16[8,24,640]{2,1,0:T(8,128)(2,1)S(1)} %bitcast.14), channel_id=1, replica_groups=mesh['dp_0'=8,'dp_1'=4,'dp_2'=3,'pipe_0'=4,'pipe_1'=2] {'dp_0'}, dimensions={0} | all-to-all | bytes 491520 | tf_op jit(solution)/shard_map/all_to_all | solution.py:246
  18.5 0.0 copy-done
  18.5 1.6 %second.1 = (bf16[288,640]{1,0:T(8,128)(2,1)S(1)}, f32[8,128]{1,0:T(8,128)S(1)}) custom-call(bf16[192,640]{1,0:T(8,128)(2,1)} %bitcast.18, f32[8,128]{1,0:T(8,128)} %copy-done), custom_call_target="tpu_custom_call" | custom-call | tf_op jit(solution)/shard_map/second/pallas_call | solution.py:247
  20.1 0.0 copy-start.1
  20.2 29.2 %all_to_all.33 = bf16[12,24,640]{2,1,0:T(8,128)(2,1)S(1)} all-to-all(bf16[12,24,640]{2,1,0:T(8,128)(2,1)S(1)} %bitcast.13), channel_id=1, replica_groups=mesh['dp_0'=8,'dp_1'=4,'dp_2'=3,'pipe_0'=4,'pipe_1'=2] {'dp_2','dp_1'}, dimensions={0} | all-to-all | bytes 737280 | tf_op jit(solution)/shard_map/all_to_all | solution.py:250
  49.4 0.0 copy-done.1
  49.4 1.2 %squares.1 = f32[64,1,128]{2,1,0:T(1,128)S(1)} custom-call(bf16[288,640]{1,0:T(8,128)(2,1)S(1)} %bitcast.15, f32[8,128]{1,0:T(8,128)} %copy-done.1), custom_call_target="tpu_custom_call" | custom-call | tf_op jit(solution)/shard_map/squares/pallas_call | solution.py:252
  50.6 20.7 %all_to_all.34 = f32[64,1,128]{2,1,0:T(1,128)S(1)} all-to-all(f32[64,1,128]{2,1,0:T(1,128)S(1)} %squares.1), channel_id=1, replica_groups=mesh['dp_0'=8,'dp_1'=4,'dp_2'=3,'pipe_0'=4,'pipe_1'=2] {'dp_0','dp_1','p..., dimensions={0} | all-to-all | bytes 65536 | tf_op jit(solution)/shard_map/all_to_all | solution.py:253
  71.2 0.1 reduce_sum.27
  71.3 0.6 broadcast_in_dim.4
  71.9 5.0 %all-to-all-start.3 = ((f32[12,1,128]{2,1,0:T(1,128)}), f32[12,1,128]{2,1,0:T(1,128)S(1)}, u32[]{:S(2)}, u32[]{:S(2)}) async-start(f32[12,1,128]{2,1,0:T(1,128)} %broadcast_in_dim.4), calls=%async_computation.3 | async-start | bytes 12288 | tf_op jit(solution)/shard_map/all_to_all | solution.py:255
  76.9 8.9 %all-to-all-done.3 = f32[12,1,128]{2,1,0:T(1,128)S(1)} async-done(((f32[12,1,128]{2,1,0:T(1,128)}), f32[12,1,128]{2,1,0:T(1,128)S(1)}, u32[]{:S(2)}, u32[]{:S(2)}) %all-to-all-start.3) | async-done | bytes 6176 | tf_op jit(solution)/shard_map/all_to_all | solution.py:255
  85.8 0.7 slice_reduce_fusion
  87.1 2.5 %conditional.1 = (f32[1408,576]{0,1:T(8,128)}) conditional(s32[]{:T(128)} %convert_element_type.6, (bf16[288,640]{1,0:T(8,128)(2,1)S(1)}, f32[12,1,128]{2,1,0:T(1,128)S(1)}) %tuple.73, (bf16[64,576]{1,0:T(8,128)(2,1)}, s32[64]{0:T(128)}) %tuple.24), branch_computations={%region_2.0_spmd, %region_3.16_spmd} | conditional | flops 118767696 | bytes 28786664 | solution.py:268
  87.1 2.5 %rows.1 = f32[576,1408]{1,0:T(8,128)} custom-call(bf16[288,640]{1,0:T(8,128)(2,1)S(1)} %get-tuple-element.76.rows_ref, f32[12,1,128]{2,1,0:T(1,128)S(1)} %get-tuple-element.77.parts_ref), custom_call_target="tpu_custom_call" | custom-call | tf_op jit(solution)/shard_map/cond/branch_0_fun/rows/pallas_call | solution.py:259
Async XLA Ops:
  1.8 16.7 %copy-start = (f32[8,128]{1,0:T(8,128)}, f32[8,128]{1,0:T(8,128)S(1)}, u32[]{:S(2)}) copy-start(f32[8,128]{1,0:T(8,128)S(1)} %get-tuple-element.110.over_in_ref) | copy-start | bytes 12292
  20.1 29.2 %copy-start.1 = (f32[8,128]{1,0:T(8,128)}, f32[8,128]{1,0:T(8,128)S(1)}, u32[]{:S(2)}) copy-start(f32[8,128]{1,0:T(8,128)S(1)} %get-tuple-element.112.over_ref) | copy-start | bytes 12292
  71.9 13.9 %all-to-all-start.3 = ((f32[12,1,128]{2,1,0:T(1,128)}), f32[12,1,128]{2,1,0:T(1,128)S(1)}, u32[]{:S(2)}, u32[]{:S(2)}) async-start(f32[12,1,128]{2,1,0:T(1,128)} %broadcast_in_dim.4), calls=%async_computation.3 | async-start | bytes 12288 | tf_op jit(solution)/shard_map/all_to_all | solution.py:255

commit v3 on v2

--- a/solution.py
+++ b/solution.py
@@ -23,7 +23,8 @@
 FIRST = (Y,)
 FIRST_CAP = 24
 SECOND = (ZH, X)
-SECOND_CAP = 24
+SECOND_CAP = 16
+FAR = 4096.0
 NORM_1 = (Y, X, CORE)
 NORM_2 = (ZH, ZL)
 
@@ -76,7 +77,7 @@
     return jnp.where(lane == AUX, high, jnp.where(lane == AUX + 1, middle, jnp.where(lane == AUX + 2, low, 0.0)))
 
 
-def pack(code_row, code_col, axes, cap):
+def pack(code_row, code_col, axes):
     n = code_row.shape[1]
     i, j = square_iota(n)
     real_row = code_row > 0.5
@@ -93,16 +94,22 @@
     before = jnp.sum(jnp.where((to_col == to_row) & (j < i), width_row, 0.0), axis=1, keepdims=True)
     before = jnp.where(lead_col, before, 0.0)
     slot_in = jnp.sum(same * before, axis=0, keepdims=True)
-    over = jnp.max(jnp.where(real_row & (slot_in + jnp.minimum(count_row, 2.0) > cap), 1.0, 0.0), axis=1, keepdims=True)
-    base = jnp.where(real_row, to_row * cap + slot_in, -2.0)
-    return base, count_row, lead_row, over
-
-
-def fill(out_ref, base, count_row, lead_row, code_row, head, tail, slots):
-    n = base.shape[1]
-    slot = lax.broadcasted_iota(jnp.int32, (slots, n), 0).astype(F32)
-    first = slot == base
-    second = (slot == base + 1.0) & (count_row > 1.5)
+    most = jnp.max(jnp.where(real_row, slot_in + jnp.minimum(count_row, 2.0), 0.0), axis=1, keepdims=True)
+    return to_row, slot_in, count_row, lead_row, most
+
+
+def fill(out_ref, where, cap, turn, code_row, head, tail):
+    to_row, slot_in, count_row, lead_row, _ = where
+    slots = out_ref.shape[0]
+    slot = lax.broadcasted_iota(jnp.int32, (slots, to_row.shape[1]), 0).astype(F32)
+    slot_in = slot_in - float(turn * cap)
+
+    def at(place_in, valid):
+        fits = valid & (to_row > -0.5) & (place_in > -0.5) & (place_in < cap - 0.5)
+        return slot == jnp.where(fits, to_row * cap + place_in, -1.0)
+
+    first = at(slot_in, True)
+    second = at(slot_in + 1.0, count_row > 1.5)
     take = jnp.where(first | second, 1.0, 0.0)
     code = jnp.sum(jnp.where(lead_row, take * code_row, 0.0), axis=1, keepdims=True)
     is_second = jnp.max(jnp.where(second, 1.0, 0.0), axis=1, keepdims=True) > 0.5
@@ -123,21 +130,22 @@
     load.start()
     code_row = ids_ref[...].astype(F32) + 1.0
     code_col = row_to_column(code_row)
-    slots = out_ref.shape[0]
-    base, count, lead, over = pack(code_row, code_col, FIRST, FIRST_CAP)
-    over_ref[...] = jnp.broadcast_to(over, over_ref.shape)
+    where = pack(code_row, code_col, FIRST)
+    over_ref[...] = jnp.broadcast_to(jnp.where(where[-1] > FIRST_CAP, FAR, 0.0), over_ref.shape)
     load.wait()
     tail = grad_ref[:, TAIL:]
     tail = jnp.concatenate([tail, jnp.zeros_like(tail)], axis=1)
-    fill(out_ref, base, count, lead, code_row, grad_ref[:, :TAIL], tail, slots)
-
-
-def second_kernel(rows_ref, over_in_ref, out_ref, over_ref):
+    fill(out_ref, where, FIRST_CAP, 0, code_row, grad_ref[:, :TAIL], tail)
+
+
+def second_kernel(rows_ref, over_in_ref, out_ref, over_ref, *, turn):
     tail = rows_ref[:, TAIL:]
     code_col = decode(tail)
     code_row = column_to_row(code_col)
-    base, count, lead, over = pack(code_row, code_col, SECOND, SECOND_CAP)
-    fill(out_ref, base, count, lead, code_row, rows_ref[:, :TAIL], tail, out_ref.shape[0])
+    where = pack(code_row, code_col, SECOND)
+    fill(out_ref, where, SECOND_CAP, turn, code_row, rows_ref[:, :TAIL], tail)
+    more = where[-1]
+    over = jnp.where(more > 2 * SECOND_CAP, FAR, jnp.where(more > SECOND_CAP, 1.0, 0.0))
     over_ref[...] = jnp.broadcast_to(over, over_ref.shape) + over_in_ref[...]
 
 
@@ -166,7 +174,11 @@
     return jnp.minimum(1.0, 0.2 * math.sqrt(tokens * D) / grad_norm)
 
 
-EDGES = (0, 384, 768, 1152, VOC_DEV)
+def relay_kernel(parts_ref, out_ref):
+    out_ref[...] = jnp.broadcast_to(jnp.sum(parts_ref[...], axis=0, keepdims=True), out_ref.shape)
+
+
+EDGES = (0, 256, 512, 768, 1024, 1280, VOC_DEV)
 
 
 def write_kernel(rows_ref, parts_ref, out_hbm, made_ref, sems, *, tokens):
@@ -231,11 +243,35 @@
     return summed * (clip_factor(total, tokens * 96) * math.sqrt(D))
 
 
+def kernel(body, out_shape, name, **more):
+    vmem = pl.BlockSpec(memory_space=pltpu.VMEM)
+
+    def call(*arrays):
+        held = [pltpu.with_memory_space_constraint(a, pltpu.VMEM) for a in arrays]
+        return pl.pallas_call(body, in_specs=[vmem] * len(held), out_shape=out_shape, name=name, **more)(*held)
+
+    return call
+
+
+def send_on(held, over, turn):
+    slots = axis_size(SECOND) * SECOND_CAP
+    body = functools.partial(second_kernel, turn=turn)
+    sent, over = kernel(body, (near((slots, WIDE), BF16), near((8, 128))), "second")(held, over)
+    return lax.all_to_all(sent, SECOND, 0, 0, tiled=True), over
+
+
+def norm_parts(rows, over):
+    n1, n2 = axis_size(NORM_1), axis_size(NORM_2)
+    part = kernel(norm_kernel, near((n1, 1, 128)), "squares")(rows, over)
+    part = lax.all_to_all(part, NORM_1, 0, 0, tiled=True)
+    part = kernel(relay_kernel, near((n2, 1, 128)), "relay")(part)
+    return lax.all_to_all(part, NORM_2, 0, 0, tiled=True)
+
+
 def per_device(embed_grad, ids):
     tokens = ids.shape[0]
     cols = embed_grad.shape[1]
     slots_1 = axis_size(FIRST) * FIRST_CAP
-    slots_2 = axis_size(SECOND) * SECOND_CAP
     sent, over = pl.pallas_call(
         first_kernel,
         in_specs=[pl.BlockSpec(memory_space=pltpu.HBM), pl.BlockSpec(memory_space=pltpu.VMEM)],
@@ -244,28 +280,27 @@
         name="first",
     )(pltpu.with_memory_space_constraint(embed_grad, pltpu.HBM), ids.reshape(1, tokens))
     held = lax.all_to_all(sent, FIRST, 0, 0, tiled=True)
-    sent, over = pl.pallas_call(second_kernel, out_shape=(near((slots_2, WIDE), BF16), near((8, 128))), name="second")(
-        held, over
-    )
-    held = lax.all_to_all(sent, SECOND, 0, 0, tiled=True)
-    n1, n2 = axis_size(NORM_1), axis_size(NORM_2)
-    part = pl.pallas_call(norm_kernel, out_shape=near((n1, 1, 128)), name="squares")(held, over)
-    part = lax.all_to_all(part, NORM_1, 0, 0, tiled=True)
-    part = jnp.broadcast_to(jnp.sum(part, axis=0, keepdims=True), (n2, 1, 128))
-    part = lax.all_to_all(part, NORM_2, 0, 0, tiled=True)
-    overflow = jnp.sum(part[:, 0, 1])
-
-    def routed():
-        return pl.pallas_call(
+    rows, over_all = send_on(held, over, 0)
+    parts = norm_parts(rows, over_all)
+
+    def written(rows, parts):
+        return kernel(
             functools.partial(write_kernel, tokens=tokens * 96),
-            in_specs=[pl.BlockSpec(memory_space=pltpu.VMEM)] * 2,
+            shape(cols, VOC_DEV),
+            "rows",
             out_specs=pl.BlockSpec(memory_space=pltpu.HBM),
-            out_shape=shape(cols, VOC_DEV),
             scratch_shapes=[pltpu.VMEM((cols, VOC_DEV), F32), pltpu.SemaphoreType.DMA((len(EDGES) - 1,))],
-            name="rows",
-        )(held, part).T
-
-    return lax.cond(overflow > 0.0, lambda: general(embed_grad, ids), routed)
+        )(rows, parts).T
+
+    def longer():
+        def extra():
+            more, over_more = send_on(held, over, 1)
+            both = jnp.concatenate([rows, more], axis=0)
+            return written(both, norm_parts(both, over_more))
+
+        return lax.cond(jnp.sum(parts[:, 0, 1]) > FAR - 0.5, lambda: general(embed_grad, ids), extra)
+
+    return lax.cond(jnp.any(parts[:, 0, 1] > 0.5), longer, lambda: written(rows, parts))
 
 
 def solution(mesh):

time: 90 us -> 83.2 us (0.924)
  blocking collectives: 66.6 us -> 76.5 us
  waiting for transfers between devices: 8.87 us -> 0 us
  starting transfers between devices: 4.99 us -> 0 us
  Pallas kernels: 7.06 us -> 4.97 us
    all_to_all x2 -> x3, blocking collectives: 49.9 us -> 59.9 us  [the longest x1 27 us: send_on(): return (lax.all_to_all(sent, SECOND, 0, 0, tiled=True), over)]
    all_to_all x1 -> x0, waiting for transfers between devices: 8.87 us -> none  [per_device(): part = lax.all_to_all(part, NORM_2, 0, 0, tiled=True)]
    all_to_all x1 -> x0, starting transfers between devices: 4.99 us -> none  [per_device(): part = lax.all_to_all(part, NORM_2, 0, 0, tiled=True)]
    pallas_call x3 -> x4, Pallas kernels: 5.27 us -> 3.19 us  [call(): pl.pallas_call(body, in_specs=[vmem] * len(held), out_shape=out_shape, na...]
  transfers between devices with their start and end apart: 1 -> 0, of which waited for: 1 -> 0; matrix products, arithmetic and copies ran while one was open for 0% -> 0% of each run, Pallas kernels for 0% -> 0%
where the time goes in v3:
time: 83.2 us; the launch traced here: 82.9 us
  blocking collectives  76.5 us (92%)
  Pallas kernels  4.97 us (6%)
    all_to_all x1, blocking collectives, send_on(): return (lax.all_to_all(sent, SECOND, 0, 0, tiled=True), over)  27 us
    all_to_all x1, blocking collectives, norm_parts(): part = lax.all_to_all(part, NORM_1, 0, 0, tiled=True)  20.1 us
    all_to_all x1, blocking collectives, per_device(): held = lax.all_to_all(sent, FIRST, 0, 0, tiled=True)  16.6 us
    all_to_all x1, blocking collectives, norm_parts(): return lax.all_to_all(part, NORM_2, 0, 0, tiled=True)  12.8 us
    pallas_call x4, Pallas kernels, call(): pl.pallas_call(body, in_specs=[vmem] * len(held), out_shape=out_shape, na...  3.19 us
    pallas_call x1, Pallas kernels, per_device(): pl.pallas_call(first_kernel, in_specs=[pl.BlockSpec(memory_space=pltpu.HB...  1.78 us

profile of v3, /device:TPU:1, one launch (start us, length us, event | category | flops | bytes accessed | tf_op | source)
XLA Modules:
  0.0 82.9 jit_solution(5067563695938995528)
XLA Ops:
  0.0 1.8 %first.1 = (bf16[192,640]{1,0:T(8,128)(2,1)S(1)}, f32[8,128]{1,0:T(8,128)S(1)}) custom-call(bf16[64,576]{1,0:T(8,128)(2,1)} %grad_hbm.1, s32[1,64]{1,0:T(1,128)} %bitcast.27), custom_call_target="tpu_custom_call" | custom-call | tf_op jit(solution)/shard_map/first/pallas_call | solution.py:275
  1.8 16.6 %all_to_all.52 = bf16[8,24,640]{2,1,0:T(8,128)(2,1)S(1)} all-to-all(bf16[8,24,640]{2,1,0:T(8,128)(2,1)S(1)} %bitcast.21), channel_id=1, replica_groups=mesh['dp_0'=8,'dp_1'=4,'dp_2'=3,'pipe_0'=4,'pipe_1'=2] {'dp_0'}, dimensions={0} | all-to-all | bytes 491520 | tf_op jit(solution)/shard_map/all_to_all | solution.py:282
  18.4 0.0 copy-start
  18.4 0.6 second.3
  19.0 27.0 %all_to_all.53 = bf16[12,16,640]{2,1,0:T(8,128)(2,1)S(1)} all-to-all(bf16[12,16,640]{2,1,0:T(8,128)(2,1)S(1)} %bitcast.22), channel_id=1, replica_groups=mesh['dp_0'=8,'dp_1'=4,'dp_2'=3,'pipe_0'=4,'pipe_1'=2] {'dp_2','dp_1'}, dimensions={0} | all-to-all | bytes 491520 | tf_op jit(solution)/shard_map/all_to_all | solution.py:260
  45.9 0.4 squares.3
  46.3 20.1 %all_to_all.54.parts_ref = f32[64,1,128]{2,1,0:T(1,128)S(1)} all-to-all(f32[64,1,128]{2,1,0:T(1,128)S(1)} %squares.3), channel_id=1, replica_groups=mesh['dp_0'=8,'dp_1'=4,'dp_2'=3,'pipe_0'=4,'pipe_1'=2] {'dp_0','dp_1','p..., dimensions={0} | all-to-all | bytes 65536 | tf_op jit(solution)/shard_map/all_to_all | solution.py:266
  66.5 0.1 relay.3
  66.5 12.8 %all_to_all.55 = f32[12,1,128]{2,1,0:T(1,128)S(1)} all-to-all(f32[12,1,128]{2,1,0:T(1,128)S(1)} %relay.3), channel_id=1, replica_groups=mesh['dp_0'=8,'dp_1'=4,'dp_2'=3,'pipe_0'=4,'pipe_1'=2] {'dp_2','pipe_0'}, dimensions={0} | all-to-all | bytes 12288 | tf_op jit(solution)/shard_map/all_to_all | solution.py:268
  79.3 0.7 compare_reduce_fusion
  80.7 0.0 copy-done
  80.7 2.2 %conditional.2 = (f32[1408,576]{0,1:T(8,128)}) conditional(s32[]{:T(128)} %convert_element_type.9, (bf16[192,640]{1,0:T(8,128)(2,1)S(1)}, f32[12,1,128]{2,1,0:T(1,128)S(1)}) %tuple.81, (f32[12,1,128]{2,1,0:T(1,128)S(1)}, bf16[192,640]{1,0:T(8,128)(2,1)}, f32[8,128]{1,0:T(8,128)S(1)}, bf16[192,640]{1,0:T(8,128)(2,1)S(1)}, bf16[64,576]{1,0:T(8,128)(2,1)}, ...), branch_computations={%region_1.0_spmd, %region_2.18_spmd} | conditional | flops 118767712 | bytes 28786778 | solution.py:303
  80.7 2.2 %rows.2 = f32[576,1408]{1,0:T(8,128)} custom-call(bf16[192,640]{1,0:T(8,128)(2,1)S(1)} %get-tuple-element.96.rows_ref, f32[12,1,128]{2,1,0:T(1,128)S(1)} %get-tuple-element.98.parts_ref), custom_call_target="tpu_custom_call" | custom-call | tf_op jit(solution)/shard_map/cond/branch_0_fun/rows/pallas_call | solution.py:251
Async XLA Ops:
  18.4 62.3 %copy-start = (bf16[8,24,640]{2,1,0:T(8,128)(2,1)}, bf16[8,24,640]{2,1,0:T(8,128)(2,1)S(1)}, u32[]{:S(2)}) copy-start(bf16[8,24,640]{2,1,0:T(8,128)(2,1)S(1)} %all_to_all.52) | copy-start | bytes 737284

commit v4 on v3

--- a/solution.py
+++ b/solution.py
@@ -125,9 +125,12 @@
     out_ref[:, TAIL:] = jnp.where(lane < AUX, split(tail), encode(code)).astype(BF16)
 
 
-def first_kernel(grad_hbm, ids_ref, out_ref, over_ref, grad_ref, sem):
-    load = pltpu.make_async_copy(grad_hbm, grad_ref, sem)
+def first_kernel(grad_hbm, ids_hbm, out_ref, over_ref, grad_ref, ids_ref, sems):
+    load_ids = pltpu.make_async_copy(ids_hbm, ids_ref, sems.at[0])
+    load = pltpu.make_async_copy(grad_hbm, grad_ref, sems.at[1])
+    load_ids.start()
     load.start()
+    load_ids.wait()
     code_row = ids_ref[...].astype(F32) + 1.0
     code_col = row_to_column(code_row)
     where = pack(code_row, code_col, FIRST)
@@ -181,11 +184,12 @@
 EDGES = (0, 256, 512, 768, 1024, 1280, VOC_DEV)
 
 
-def write_kernel(rows_ref, parts_ref, out_hbm, made_ref, sems, *, tokens):
+def write_kernel(rows_ref, parts_ref, out_hbm, short_ref, made_ref, sems, *, tokens):
     turned = rows_ref[...].T[: made_ref.shape[0], :]
     lane = lax.broadcasted_iota(jnp.int32, (1, 128), 1)
-    total = jnp.sum(parts_ref[...], axis=0)
-    total = jnp.sum(jnp.where(lane == 0, total, 0.0), axis=1, keepdims=True)
+    parts = jnp.sum(parts_ref[...], axis=0)
+    total = jnp.sum(jnp.where(lane == 0, parts, 0.0), axis=1, keepdims=True)
+    short_ref[0] = jnp.max(jnp.where(lane == 1, parts, 0.0)).astype(jnp.int32)
     scale = clip_factor(total, tokens) * math.sqrt(D)
     code = decode(rows_ref[:, TAIL:])
     local = code - 1.0
@@ -209,6 +213,10 @@
     return pltpu.VMEM(dims, dtype)
 
 
+def times_kernel(sums_ref, scale_ref, out_ref):
+    out_ref[...] = sums_ref[...] * scale_ref[...]
+
+
 def around(axes, sizes, value, body, init):
     if not axes:
         return value, body(value, init)
@@ -240,7 +248,8 @@
     total = jnp.sum(summed * summed)
     for axis in AXES:
         total = lax.psum(total, axis)
-    return summed * (clip_factor(total, tokens * 96) * math.sqrt(D))
+    scale = clip_factor(total, tokens * 96) * math.sqrt(D)
+    return pl.pallas_call(times_kernel, out_shape=shape(cols, VOC_DEV), name="times")(summed.T, scale.reshape(1, 1))
 
 
 def kernel(body, out_shape, name, **more):
@@ -268,39 +277,52 @@
     return lax.all_to_all(part, NORM_2, 0, 0, tiled=True)
 
 
-def per_device(embed_grad, ids):
-    tokens = ids.shape[0]
-    cols = embed_grad.shape[1]
+def send_first(embed_grad, ids):
+    tokens, cols = embed_grad.shape
     slots_1 = axis_size(FIRST) * FIRST_CAP
+    hbm = pl.BlockSpec(memory_space=pltpu.HBM)
     sent, over = pl.pallas_call(
         first_kernel,
-        in_specs=[pl.BlockSpec(memory_space=pltpu.HBM), pl.BlockSpec(memory_space=pltpu.VMEM)],
+        in_specs=[hbm, hbm],
         out_shape=(near((slots_1, WIDE), BF16), near((8, 128))),
-        scratch_shapes=[pltpu.VMEM((tokens, cols), BF16), pltpu.SemaphoreType.DMA],
+        scratch_shapes=[
+            pltpu.VMEM((tokens, cols), BF16),
+            pltpu.VMEM((1, tokens), jnp.int32),
+            pltpu.SemaphoreType.DMA((2,)),
+        ],
         name="first",
-    )(pltpu.with_memory_space_constraint(embed_grad, pltpu.HBM), ids.reshape(1, tokens))
-    held = lax.all_to_all(sent, FIRST, 0, 0, tiled=True)
-    rows, over_all = send_on(held, over, 0)
-    parts = norm_parts(rows, over_all)
+    )(*[pltpu.with_memory_space_constraint(a, pltpu.HBM) for a in (embed_grad, ids.reshape(1, tokens))])
+    return lax.all_to_all(sent, FIRST, 0, 0, tiled=True), over
+
+
+def per_device(embed_grad, ids):
+    tokens, cols = embed_grad.shape
 
     def written(rows, parts):
         return kernel(
             functools.partial(write_kernel, tokens=tokens * 96),
-            shape(cols, VOC_DEV),
+            (shape(cols, VOC_DEV), jax.ShapeDtypeStruct((1,), jnp.int32)),
             "rows",
-            out_specs=pl.BlockSpec(memory_space=pltpu.HBM),
+            out_specs=(pl.BlockSpec(memory_space=pltpu.HBM), pl.BlockSpec(memory_space=pltpu.SMEM)),
             scratch_shapes=[pltpu.VMEM((cols, VOC_DEV), F32), pltpu.SemaphoreType.DMA((len(EDGES) - 1,))],
-        )(rows, parts).T
-
-    def longer():
+        )(rows, parts)
+
+    def again(state):
         def extra():
-            more, over_more = send_on(held, over, 1)
+            held, over = send_first(embed_grad, ids)
+            rows, over_all = send_on(held, over, 0)
+            more, _ = send_on(held, over, 1)
             both = jnp.concatenate([rows, more], axis=0)
-            return written(both, norm_parts(both, over_more))
-
-        return lax.cond(jnp.sum(parts[:, 0, 1]) > FAR - 0.5, lambda: general(embed_grad, ids), extra)
-
-    return lax.cond(jnp.any(parts[:, 0, 1] > 0.5), longer, lambda: written(rows, parts))
+            return written(both, norm_parts(both, over_all))[0]
+
+        out = lax.cond(state[1] >= int(FAR), lambda: general(embed_grad, ids), extra)
+        return out, jnp.int32(0)
+
+    held, over = send_first(embed_grad, ids)
+    rows, over = send_on(held, over, 0)
+    out, short = written(rows, norm_parts(rows, over))
+    out, _ = lax.while_loop(lambda state: state[1] > 0, again, (out, short[0]))
+    return out.T
 
 
 def solution(mesh):

time: 83.2 us -> 82.4 us (level)
  no operation moved by 1% of the time
where the time goes in v4:
time: 82.4 us; the launch traced here: 82.1 us
  blocking collectives  76.5 us (93%)
  Pallas kernels  4.89 us (6%)
    all_to_all x1, blocking collectives, send_on(): return (lax.all_to_all(sent, SECOND, 0, 0, tiled=True), over)  27 us
    all_to_all x1, blocking collectives, norm_parts(): part = lax.all_to_all(part, NORM_1, 0, 0, tiled=True)  20.1 us
    all_to_all x1, blocking collectives, send_first(): return (lax.all_to_all(sent, FIRST, 0, 0, tiled=True), over)  16.6 us
    all_to_all x1, blocking collectives, norm_parts(): return lax.all_to_all(part, NORM_2, 0, 0, tiled=True)  12.8 us
    pallas_call x4, Pallas kernels, call(): pl.pallas_call(body, in_specs=[vmem] * len(held), out_shape=out_shape, na...  3.71 us

profile of v4, /device:TPU:1, one launch (start us, length us, event | category | flops | bytes accessed | tf_op | source)
XLA Modules:
  0.0 82.1 jit_solution(7622517032314053939)
XLA Ops:
  0.0 1.2 %first.3 = (bf16[192,640]{1,0:T(8,128)(2,1)S(1)}, f32[8,128]{1,0:T(8,128)S(1)}) custom-call(bf16[64,576]{1,0:T(8,128)(2,1)} %grad_hbm.1, s32[1,64]{1,0:T(1,128)} %bitcast.35), custom_call_target="tpu_custom_call" | custom-call | tf_op jit(solution)/shard_map/first/pallas_call | solution.py:284
  1.2 16.6 %all_to_all.70 = bf16[8,24,640]{2,1,0:T(8,128)(2,1)S(1)} all-to-all(bf16[8,24,640]{2,1,0:T(8,128)(2,1)S(1)} %bitcast.32), channel_id=1, replica_groups=mesh['dp_0'=8,'dp_1'=4,'dp_2'=3,'pipe_0'=4,'pipe_1'=2] {'dp_0'}, dimensions={0} | all-to-all | bytes 491520 | tf_op jit(solution)/shard_map/all_to_all | solution.py:295
  17.8 0.6 second.5
  18.4 27.0 %all_to_all.71 = bf16[12,16,640]{2,1,0:T(8,128)(2,1)S(1)} all-to-all(bf16[12,16,640]{2,1,0:T(8,128)(2,1)S(1)} %bitcast.31), channel_id=1, replica_groups=mesh['dp_0'=8,'dp_1'=4,'dp_2'=3,'pipe_0'=4,'pipe_1'=2] {'dp_2','dp_1'}, dimensions={0} | all-to-all | bytes 491520 | tf_op jit(solution)/shard_map/all_to_all | solution.py:269
  45.3 0.4 squares.3
  45.7 20.1 %all_to_all.72.parts_ref = f32[64,1,128]{2,1,0:T(1,128)S(1)} all-to-all(f32[64,1,128]{2,1,0:T(1,128)S(1)} %squares.3), channel_id=1, replica_groups=mesh['dp_0'=8,'dp_1'=4,'dp_2'=3,'pipe_0'=4,'pipe_1'=2] {'dp_0','dp_1','p..., dimensions={0} | all-to-all | bytes 65536 | tf_op jit(solution)/shard_map/all_to_all | solution.py:275
  65.9 0.1 relay.3
  65.9 12.8 %all_to_all.73.parts_ref = f32[12,1,128]{2,1,0:T(1,128)S(1)} all-to-all(f32[12,1,128]{2,1,0:T(1,128)S(1)} %relay.3), channel_id=1, replica_groups=mesh['dp_0'=8,'dp_1'=4,'dp_2'=3,'pipe_0'=4,'pipe_1'=2] {'dp_2','pipe_0'}, dimensions={0} | all-to-all | bytes 12288 | tf_op jit(solution)/shard_map/all_to_all | solution.py:277
  78.7 2.7 %rows.3 = (f32[576,1408]{1,0:T(8,128)}, s32[1]{0:T(128)}) custom-call(bf16[192,640]{1,0:T(8,128)(2,1)S(1)} %bitcast.29, f32[12,1,128]{2,1,0:T(1,128)S(1)} %all_to_all.73.parts_ref), custom_call_target="tpu_custom_call" | custom-call | tf_op jit(solution)/shard_map/rows/pallas_call | solution.py:260
  81.4 0.7 while.64

commit v5 on v4

--- a/solution.py
+++ b/solution.py
@@ -22,7 +22,7 @@
 
 FIRST = (Y,)
 FIRST_CAP = 24
-SECOND = (ZH, X)
+SECOND = (X, ZH)
 SECOND_CAP = 16
 FAR = 4096.0
 NORM_1 = (Y, X, CORE)
@@ -184,17 +184,18 @@
 EDGES = (0, 256, 512, 768, 1024, 1280, VOC_DEV)
 
 
-def write_kernel(rows_ref, parts_ref, out_hbm, short_ref, made_ref, sems, *, tokens):
+def write_kernel(rows_ref, parts_ref, out_hbm, short_hbm, made_ref, short_ref, sems, *, tokens):
     turned = rows_ref[...].T[: made_ref.shape[0], :]
     lane = lax.broadcasted_iota(jnp.int32, (1, 128), 1)
     parts = jnp.sum(parts_ref[...], axis=0)
     total = jnp.sum(jnp.where(lane == 0, parts, 0.0), axis=1, keepdims=True)
     short_ref[0] = jnp.max(jnp.where(lane == 1, parts, 0.0)).astype(jnp.int32)
+    copies = [pltpu.make_async_copy(short_ref, short_hbm, sems.at[len(EDGES) - 1])]
+    copies[0].start()
     scale = clip_factor(total, tokens) * math.sqrt(D)
     code = decode(rows_ref[:, TAIL:])
     local = code - 1.0
     local = jnp.where(code > 0.5, local - VOC_DEV * floor_div(local, VOC_DEV), -1.0).astype(jnp.int32)
-    copies = []
     for k, (low, high) in enumerate(zip(EDGES[:-1], EDGES[1:])):
         here = lax.broadcasted_iota(jnp.int32, (local.shape[0], high - low), 1) + low
         pick = jnp.where(here == local, 1.0, 0.0).astype(BF16)
@@ -303,8 +304,12 @@
             functools.partial(write_kernel, tokens=tokens * 96),
             (shape(cols, VOC_DEV), jax.ShapeDtypeStruct((1,), jnp.int32)),
             "rows",
-            out_specs=(pl.BlockSpec(memory_space=pltpu.HBM), pl.BlockSpec(memory_space=pltpu.SMEM)),
-            scratch_shapes=[pltpu.VMEM((cols, VOC_DEV), F32), pltpu.SemaphoreType.DMA((len(EDGES) - 1,))],
+            out_specs=(pl.BlockSpec(memory_space=pltpu.HBM),) * 2,
+            scratch_shapes=[
+                pltpu.VMEM((cols, VOC_DEV), F32),
+                pltpu.SMEM((1,), jnp.int32),
+                pltpu.SemaphoreType.DMA((len(EDGES),)),
+            ],
         )(rows, parts)
 
     def again(state):

time: 82.4 us -> 81.9 us (level)
  no operation moved by 1% of the time
where the time goes in v5:
time: 81.9 us; the launch traced here: 81.6 us
  blocking collectives  76.5 us (93%)
  Pallas kernels  4.39 us (5%)
    all_to_all x1, blocking collectives, send_on(): return (lax.all_to_all(sent, SECOND, 0, 0, tiled=True), over)  27.2 us
    all_to_all x1, blocking collectives, norm_parts(): part = lax.all_to_all(part, NORM_1, 0, 0, tiled=True)  19.9 us
    all_to_all x1, blocking collectives, send_first(): return (lax.all_to_all(sent, FIRST, 0, 0, tiled=True), over)  16.6 us
    all_to_all x1, blocking collectives, norm_parts(): return lax.all_to_all(part, NORM_2, 0, 0, tiled=True)  12.8 us
    pallas_call x4, Pallas kernels, call(): pl.pallas_call(body, in_specs=[vmem] * len(held), out_shape=out_shape, na...  3.21 us

profile of v5, /device:TPU:1, one launch (start us, length us, event | category | flops | bytes accessed | tf_op | source)
XLA Modules:
  0.0 81.6 jit_solution(2680026140934539649)
XLA Ops:
  0.0 1.2 %first.3 = (bf16[192,640]{1,0:T(8,128)(2,1)S(1)}, f32[8,128]{1,0:T(8,128)S(1)}) custom-call(bf16[64,576]{1,0:T(8,128)(2,1)} %grad_hbm.1, s32[1,64]{1,0:T(1,128)} %bitcast.35), custom_call_target="tpu_custom_call" | custom-call | tf_op jit(solution)/shard_map/first/pallas_call | solution.py:285
  1.2 16.6 %all_to_all.70 = bf16[8,24,640]{2,1,0:T(8,128)(2,1)S(1)} all-to-all(bf16[8,24,640]{2,1,0:T(8,128)(2,1)S(1)} %bitcast.32), channel_id=1, replica_groups=mesh['dp_0'=8,'dp_1'=4,'dp_2'=3,'pipe_0'=4,'pipe_1'=2] {'dp_0'}, dimensions={0} | all-to-all | bytes 491520 | tf_op jit(solution)/shard_map/all_to_all | solution.py:296
  17.8 0.6 second.5
  18.4 27.2 %all_to_all.71 = bf16[12,16,640]{2,1,0:T(8,128)(2,1)S(1)} all-to-all(bf16[12,16,640]{2,1,0:T(8,128)(2,1)S(1)} %bitcast.31), channel_id=1, replica_groups=mesh['dp_0'=8,'dp_1'=4,'dp_2'=3,'pipe_0'=4,'pipe_1'=2] {'dp_1','dp_2'}, dimensions={0} | all-to-all | bytes 491520 | tf_op jit(solution)/shard_map/all_to_all | solution.py:270
  45.6 0.4 squares.3
  46.0 19.9 %all_to_all.72.parts_ref = f32[64,1,128]{2,1,0:T(1,128)S(1)} all-to-all(f32[64,1,128]{2,1,0:T(1,128)S(1)} %squares.3), channel_id=1, replica_groups=mesh['dp_0'=8,'dp_1'=4,'dp_2'=3,'pipe_0'=4,'pipe_1'=2] {'dp_0','dp_1','p..., dimensions={0} | all-to-all | bytes 65536 | tf_op jit(solution)/shard_map/all_to_all | solution.py:276
  65.8 0.1 relay.3
  65.9 12.8 %all_to_all.73.parts_ref = f32[12,1,128]{2,1,0:T(1,128)S(1)} all-to-all(f32[12,1,128]{2,1,0:T(1,128)S(1)} %relay.3), channel_id=1, replica_groups=mesh['dp_0'=8,'dp_1'=4,'dp_2'=3,'pipe_0'=4,'pipe_1'=2] {'dp_2','pipe_0'}, dimensions={0} | all-to-all | bytes 12288 | tf_op jit(solution)/shard_map/all_to_all | solution.py:278
  78.7 2.2 %rows.3 = (f32[576,1408]{1,0:T(8,128)}, s32[1]{0:T(128)}) custom-call(bf16[192,640]{1,0:T(8,128)(2,1)S(1)} %bitcast.29, f32[12,1,128]{2,1,0:T(1,128)S(1)} %all_to_all.73.parts_ref), custom_call_target="tpu_custom_call" | custom-call | tf_op jit(solution)/shard_map/rows/pallas_call | solution.py:261
  80.9 0.7 while.64

commit v6 on v5

--- a/solution.py
+++ b/solution.py
@@ -25,8 +25,8 @@
 SECOND = (X, ZH)
 SECOND_CAP = 16
 FAR = 4096.0
-NORM_1 = (Y, X, CORE)
-NORM_2 = (ZH, ZL)
+NORM_1 = (ZH, ZL)
+NORM_2 = (Y, X, CORE)
 
 
 def axis_size(axes):

time: 81.9 us -> 83.3 us (1.017)
  blocking collectives: 76.5 us -> 77.9 us
    all_to_all x1, blocking collectives: 12.8 us -> 15.7 us  [norm_parts(): return lax.all_to_all(part, NORM_2, 0, 0, tiled=True)]
    all_to_all x1, blocking collectives: 19.9 us -> 18.4 us  [norm_parts(): part = lax.all_to_all(part, NORM_1, 0, 0, tiled=True)]
where the time goes in v6:
time: 83.3 us; the launch traced here: 83 us
  blocking collectives  77.9 us (94%)
  Pallas kernels  4.33 us (5%)
    all_to_all x1, blocking collectives, send_on(): return (lax.all_to_all(sent, SECOND, 0, 0, tiled=True), over)  27.2 us
    all_to_all x1, blocking collectives, norm_parts(): part = lax.all_to_all(part, NORM_1, 0, 0, tiled=True)  18.4 us
    all_to_all x1, blocking collectives, send_first(): return (lax.all_to_all(sent, FIRST, 0, 0, tiled=True), over)  16.6 us
    all_to_all x1, blocking collectives, norm_parts(): return lax.all_to_all(part, NORM_2, 0, 0, tiled=True)  15.7 us
    pallas_call x4, Pallas kernels, call(): pl.pallas_call(body, in_specs=[vmem] * len(held), out_shape=out_shape, na...  3.15 us

profile of v6, /device:TPU:1, one launch (start us, length us, event | category | flops | bytes accessed | tf_op | source)
XLA Modules:
  0.0 83.0 jit_solution(14052324374834309516)
XLA Ops:
  0.0 1.2 %first.3 = (bf16[192,640]{1,0:T(8,128)(2,1)S(1)}, f32[8,128]{1,0:T(8,128)S(1)}) custom-call(bf16[64,576]{1,0:T(8,128)(2,1)} %grad_hbm.1, s32[1,64]{1,0:T(1,128)} %bitcast.35), custom_call_target="tpu_custom_call" | custom-call | tf_op jit(solution)/shard_map/first/pallas_call | solution.py:285
  1.2 16.6 %all_to_all.70 = bf16[8,24,640]{2,1,0:T(8,128)(2,1)S(1)} all-to-all(bf16[8,24,640]{2,1,0:T(8,128)(2,1)S(1)} %bitcast.32), channel_id=1, replica_groups=mesh['dp_0'=8,'dp_1'=4,'dp_2'=3,'pipe_0'=4,'pipe_1'=2] {'dp_0'}, dimensions={0} | all-to-all | bytes 491520 | tf_op jit(solution)/shard_map/all_to_all | solution.py:296
  17.8 0.6 second.5
  18.4 27.2 %all_to_all.71 = bf16[12,16,640]{2,1,0:T(8,128)(2,1)S(1)} all-to-all(bf16[12,16,640]{2,1,0:T(8,128)(2,1)S(1)} %bitcast.31), channel_id=1, replica_groups=mesh['dp_0'=8,'dp_1'=4,'dp_2'=3,'pipe_0'=4,'pipe_1'=2] {'dp_1','dp_2'}, dimensions={0} | all-to-all | bytes 491520 | tf_op jit(solution)/shard_map/all_to_all | solution.py:270
  45.6 0.4 squares.3
  46.0 18.4 %all_to_all.72.parts_ref = f32[12,1,128]{2,1,0:T(1,128)S(1)} all-to-all(f32[12,1,128]{2,1,0:T(1,128)S(1)} %squares.3), channel_id=1, replica_groups=mesh['dp_0'=8,'dp_1'=4,'dp_2'=3,'pipe_0'=4,'pipe_1'=2] {'dp_2','pipe_0'}, dimensions={0} | all-to-all | bytes 12288 | tf_op jit(solution)/shard_map/all_to_all | solution.py:276
  64.3 15.7 %all_to_all.73.parts_ref = f32[64,1,128]{2,1,0:T(1,128)S(1)} all-to-all(f32[64,1,128]{2,1,0:T(1,128)S(1)} %relay.3), channel_id=1, replica_groups=mesh['dp_0'=8,'dp_1'=4,'dp_2'=3,'pipe_0'=4,'pipe_1'=2] {'dp_0','dp_1','p..., dimensions={0} | all-to-all | bytes 65536 | tf_op jit(solution)/shard_map/all_to_all | solution.py:278
  80.1 2.2 %rows.3 = (f32[576,1408]{1,0:T(8,128)}, s32[1]{0:T(128)}) custom-call(bf16[192,640]{1,0:T(8,128)(2,1)S(1)} %bitcast.29, f32[64,1,128]{2,1,0:T(1,128)S(1)} %all_to_all.73.parts_ref), custom_call_target="tpu_custom_call" | custom-call | tf_op jit(solution)/shard_map/rows/pallas_call | solution.py:261
  82.3 0.7 while.64
  (1 shorter events, 0.0 us)

commit v7 on v6

--- a/solution.py
+++ b/solution.py
@@ -25,8 +25,8 @@
 SECOND = (X, ZH)
 SECOND_CAP = 16
 FAR = 4096.0
-NORM_1 = (ZH, ZL)
-NORM_2 = (Y, X, CORE)
+NORM_1 = (ZH, ZL, CORE)
+NORM_2 = (Y, X)
 
 
 def axis_size(axes):

time: 83.3 us -> 81.4 us (0.977)
  blocking collectives: 77.9 us -> 76.1 us
    all_to_all x1, blocking collectives: 15.7 us -> 11.7 us  [norm_parts(): return lax.all_to_all(part, NORM_2, 0, 0, tiled=True)]
    all_to_all x1, blocking collectives: 18.4 us -> 20.5 us  [norm_parts(): part = lax.all_to_all(part, NORM_1, 0, 0, tiled=True)]
where the time goes in v7:
time: 81.4 us; the launch traced here: 81.1 us
  blocking collectives  76.1 us (93%)
  Pallas kernels  4.34 us (5%)
    all_to_all x1, blocking collectives, send_on(): return (lax.all_to_all(sent, SECOND, 0, 0, tiled=True), over)  27.2 us
    all_to_all x1, blocking collectives, norm_parts(): part = lax.all_to_all(part, NORM_1, 0, 0, tiled=True)  20.5 us
    all_to_all x1, blocking collectives, send_first(): return (lax.all_to_all(sent, FIRST, 0, 0, tiled=True), over)  16.6 us
    all_to_all x1, blocking collectives, norm_parts(): return lax.all_to_all(part, NORM_2, 0, 0, tiled=True)  11.7 us
    pallas_call x4, Pallas kernels, call(): pl.pallas_call(body, in_specs=[vmem] * len(held), out_shape=out_shape, na...  3.16 us

profile of v7, /device:TPU:1, one launch (start us, length us, event | category | flops | bytes accessed | tf_op | source)
XLA Modules:
  0.0 81.1 jit_solution(501596818682933509)
XLA Ops:
  0.0 1.2 %first.3 = (bf16[192,640]{1,0:T(8,128)(2,1)S(1)}, f32[8,128]{1,0:T(8,128)S(1)}) custom-call(bf16[64,576]{1,0:T(8,128)(2,1)} %grad_hbm.1, s32[1,64]{1,0:T(1,128)} %bitcast.35), custom_call_target="tpu_custom_call" | custom-call | tf_op jit(solution)/shard_map/first/pallas_call | solution.py:285
  1.2 16.6 %all_to_all.70 = bf16[8,24,640]{2,1,0:T(8,128)(2,1)S(1)} all-to-all(bf16[8,24,640]{2,1,0:T(8,128)(2,1)S(1)} %bitcast.32), channel_id=1, replica_groups=mesh['dp_0'=8,'dp_1'=4,'dp_2'=3,'pipe_0'=4,'pipe_1'=2] {'dp_0'}, dimensions={0} | all-to-all | bytes 491520 | tf_op jit(solution)/shard_map/all_to_all | solution.py:296
  17.8 0.6 second.5
  18.4 27.2 %all_to_all.71 = bf16[12,16,640]{2,1,0:T(8,128)(2,1)S(1)} all-to-all(bf16[12,16,640]{2,1,0:T(8,128)(2,1)S(1)} %bitcast.31), channel_id=1, replica_groups=mesh['dp_0'=8,'dp_1'=4,'dp_2'=3,'pipe_0'=4,'pipe_1'=2] {'dp_1','dp_2'}, dimensions={0} | all-to-all | bytes 491520 | tf_op jit(solution)/shard_map/all_to_all | solution.py:270
  45.6 0.4 squares.3
  46.0 20.5 %all_to_all.72.parts_ref = f32[24,1,128]{2,1,0:T(1,128)S(1)} all-to-all(f32[24,1,128]{2,1,0:T(1,128)S(1)} %squares.3), channel_id=1, replica_groups=mesh['dp_0'=8,'dp_1'=4,'dp_2'=3,'pipe_0'=4,'pipe_1'=2] {'dp_2','pipe_0',..., dimensions={0} | all-to-all | bytes 24576 | tf_op jit(solution)/shard_map/all_to_all | solution.py:276
  66.5 11.7 %all_to_all.73.parts_ref = f32[32,1,128]{2,1,0:T(1,128)S(1)} all-to-all(f32[32,1,128]{2,1,0:T(1,128)S(1)} %relay.3), channel_id=1, replica_groups=mesh['dp_0'=8,'dp_1'=4,'dp_2'=3,'pipe_0'=4,'pipe_1'=2] {'dp_0','dp_1'}, dimensions={0} | all-to-all | bytes 32768 | tf_op jit(solution)/shard_map/all_to_all | solution.py:278
  78.2 2.2 %rows.3 = (f32[576,1408]{1,0:T(8,128)}, s32[1]{0:T(128)}) custom-call(bf16[192,640]{1,0:T(8,128)(2,1)S(1)} %bitcast.29, f32[32,1,128]{2,1,0:T(1,128)S(1)} %all_to_all.73.parts_ref), custom_call_target="tpu_custom_call" | custom-call | tf_op jit(solution)/shard_map/rows/pallas_call | solution.py:261
  80.4 0.7 while.64
  (1 shorter events, 0.0 us)

commit v8 on v7

--- a/solution.py
+++ b/solution.py
@@ -184,8 +184,16 @@
 EDGES = (0, 256, 512, 768, 1024, 1280, VOC_DEV)
 
 
-def write_kernel(rows_ref, parts_ref, out_hbm, short_hbm, made_ref, short_ref, sems, *, tokens):
-    turned = rows_ref[...].T[: made_ref.shape[0], :]
+def prepare_kernel(rows_ref, turned_ref, pick_ref):
+    turned_ref[...] = rows_ref[...].T[: turned_ref.shape[0], :]
+    code = decode(rows_ref[:, TAIL:])
+    local = code - 1.0
+    local = jnp.where(code > 0.5, local - VOC_DEV * floor_div(local, VOC_DEV), -1.0).astype(jnp.int32)
+    here = lax.broadcasted_iota(jnp.int32, pick_ref.shape, 1)
+    pick_ref[...] = jnp.where(here == local, 1.0, 0.0).astype(BF16)
+
+
+def write_kernel(turned_ref, pick_ref, parts_ref, out_hbm, short_hbm, made_ref, short_ref, sems, *, tokens):
     lane = lax.broadcasted_iota(jnp.int32, (1, 128), 1)
     parts = jnp.sum(parts_ref[...], axis=0)
     total = jnp.sum(jnp.where(lane == 0, parts, 0.0), axis=1, keepdims=True)
@@ -193,13 +201,8 @@
     copies = [pltpu.make_async_copy(short_ref, short_hbm, sems.at[len(EDGES) - 1])]
     copies[0].start()
     scale = clip_factor(total, tokens) * math.sqrt(D)
-    code = decode(rows_ref[:, TAIL:])
-    local = code - 1.0
-    local = jnp.where(code > 0.5, local - VOC_DEV * floor_div(local, VOC_DEV), -1.0).astype(jnp.int32)
     for k, (low, high) in enumerate(zip(EDGES[:-1], EDGES[1:])):
-        here = lax.broadcasted_iota(jnp.int32, (local.shape[0], high - low), 1) + low
-        pick = jnp.where(here == local, 1.0, 0.0).astype(BF16)
-        made_ref[:, low:high] = jnp.dot(turned, pick, preferred_element_type=F32) * scale
+        made_ref[:, low:high] = jnp.dot(turned_ref[...], pick_ref[:, low:high], preferred_element_type=F32) * scale
         copies.append(pltpu.make_async_copy(made_ref.at[:, low:high], out_hbm.at[:, low:high], sems.at[k]))
         copies[-1].start()
     for copy in copies:
@@ -300,6 +303,8 @@
     tokens, cols = embed_grad.shape
 
     def written(rows, parts):
+        slots = rows.shape[0]
+        made = kernel(prepare_kernel, (near((cols, slots), BF16), near((slots, VOC_DEV), BF16)), "prepare")(rows)
         return kernel(
             functools.partial(write_kernel, tokens=tokens * 96),
             (shape(cols, VOC_DEV), jax.ShapeDtypeStruct((1,), jnp.int32)),
@@ -310,7 +315,7 @@
                 pltpu.SMEM((1,), jnp.int32),
                 pltpu.SemaphoreType.DMA((len(EDGES),)),
             ],
-        )(rows, parts)
+        )(*made, parts)
 
     def again(state):
         def extra():

time: 81.4 us -> 82.5 us (1.014)
  blocking collectives: 76.1 us -> 64.3 us
  waiting for transfers between devices: 0 us -> 8.3 us
  starting transfers between devices: 0 us -> 3.83 us
    all_to_all x1 -> x0, blocking collectives: 11.7 us -> none  [norm_parts(): return lax.all_to_all(part, NORM_2, 0, 0, tiled=True)]
    all_to_all x0 -> x1, waiting for transfers between devices: none -> 8.3 us  [norm_parts(): return lax.all_to_all(part, NORM_2, 0, 0, tiled=True)]
    all_to_all x0 -> x1, starting transfers between devices: none -> 3.83 us  [norm_parts(): return lax.all_to_all(part, NORM_2, 0, 0, tiled=True)]
    pallas_call x4 -> x5, Pallas kernels: 3.16 us -> 3.88 us  [call(): pl.pallas_call(body, in_specs=[vmem] * len(held), out_shape=out_shape, na...]
  transfers between devices with their start and end apart: 0 -> 1, of which waited for: 0 -> 1; matrix products, arithmetic and copies ran while one was open for 0% -> 0% of each run, Pallas kernels for 0% -> 0%
where the time goes in v8:
time: 82.5 us; the launch traced here: 82.2 us
  blocking collectives  64.3 us (78%)
  waiting for transfers between devices  8.3 us (10%)
  Pallas kernels  5.07 us (6%)
  starting transfers between devices  3.83 us (5%)
    all_to_all x1, blocking collectives, send_on(): return (lax.all_to_all(sent, SECOND, 0, 0, tiled=True), over)  27.2 us
    all_to_all x1, blocking collectives, norm_parts(): part = lax.all_to_all(part, NORM_1, 0, 0, tiled=True)  20.5 us
    all_to_all x1, blocking collectives, send_first(): return (lax.all_to_all(sent, FIRST, 0, 0, tiled=True), over)  16.6 us
    all_to_all x1, waiting for transfers between devices, norm_parts(): return lax.all_to_all(part, NORM_2, 0, 0, tiled=True)  8.3 us
    pallas_call x5, Pallas kernels, call(): pl.pallas_call(body, in_specs=[vmem] * len(held), out_shape=out_shape, na...  3.88 us
    all_to_all x1, starting transfers between devices, norm_parts(): return lax.all_to_all(part, NORM_2, 0, 0, tiled=True)  3.83 us
  transfers between devices with their start and end apart: 1, of which 1 were waited for; matrix products, arithmetic and copies ran while one was open for 0% of the time, Pallas kernels for 0%

profile of v8, /device:TPU:1, one launch (start us, length us, event | category | flops | bytes accessed | tf_op | source)
XLA Modules:
  0.0 82.2 jit_solution(12679348544747460077)
XLA Ops:
  0.0 1.2 %first.3 = (bf16[192,640]{1,0:T(8,128)(2,1)S(1)}, f32[8,128]{1,0:T(8,128)S(1)}) custom-call(bf16[64,576]{1,0:T(8,128)(2,1)} %grad_hbm.1, s32[1,64]{1,0:T(1,128)} %bitcast.35), custom_call_target="tpu_custom_call" | custom-call | tf_op jit(solution)/shard_map/first/pallas_call | solution.py:288
  1.2 16.6 %all_to_all.69 = bf16[8,24,640]{2,1,0:T(8,128)(2,1)S(1)} all-to-all(bf16[8,24,640]{2,1,0:T(8,128)(2,1)S(1)} %bitcast.32), channel_id=1, replica_groups=mesh['dp_0'=8,'dp_1'=4,'dp_2'=3,'pipe_0'=4,'pipe_1'=2] {'dp_0'}, dimensions={0} | all-to-all | bytes 491520 | tf_op jit(solution)/shard_map/all_to_all | solution.py:299
  17.8 0.6 second.5
  18.4 27.2 %all_to_all.70 = bf16[12,16,640]{2,1,0:T(8,128)(2,1)S(1)} all-to-all(bf16[12,16,640]{2,1,0:T(8,128)(2,1)S(1)} %bitcast.31), channel_id=1, replica_groups=mesh['dp_0'=8,'dp_1'=4,'dp_2'=3,'pipe_0'=4,'pipe_1'=2] {'dp_1','dp_2'}, dimensions={0} | all-to-all | bytes 491520 | tf_op jit(solution)/shard_map/all_to_all | solution.py:273
  45.6 0.4 squares.3
  46.0 20.5 %all_to_all.71.parts_ref = f32[24,1,128]{2,1,0:T(1,128)S(1)} all-to-all(f32[24,1,128]{2,1,0:T(1,128)S(1)} %squares.3), channel_id=1, replica_groups=mesh['dp_0'=8,'dp_1'=4,'dp_2'=3,'pipe_0'=4,'pipe_1'=2] {'dp_2','pipe_0',..., dimensions={0} | all-to-all | bytes 24576 | tf_op jit(solution)/shard_map/all_to_all | solution.py:279
  66.5 0.6 relay.3
  67.1 3.8 %all-to-all-start.8 = ((f32[32,1,128]{2,1,0:T(1,128)}), f32[32,1,128]{2,1,0:T(1,128)S(1)}, u32[]{:S(2)}, u32[]{:S(2)}) async-start(f32[32,1,128]{2,1,0:T(1,128)} %relay.3), calls=%async_computation.8 | async-start | bytes 32768 | tf_op jit(solution)/shard_map/all_to_all | solution.py:281
  70.9 0.2 prepare.3
  71.2 8.3 %all-to-all-done.8.parts_ref = f32[32,1,128]{2,1,0:T(1,128)S(1)} async-done(((f32[32,1,128]{2,1,0:T(1,128)}), f32[32,1,128]{2,1,0:T(1,128)S(1)}, u32[]{:S(2)}, u32[]{:S(2)}) %all-to-all-start.8) | async-done | bytes 16416 | tf_op jit(solution)/shard_map/all_to_all | solution.py:281
  79.5 2.1 %rows.3 = (f32[576,1408]{1,0:T(8,128)}, s32[1]{0:T(128)}) custom-call(bf16[576,192]{1,0:T(8,128)(2,1)S(1)} %get-tuple-element.202.turned_ref, bf16[192,1408]{1,0:T(8,128)(2,1)S(1)} %get-tuple-element.203.pick_ref, f32[32,1,128]{2,1,0:T(1,128)S(1)} %all-to-all-done.8.parts_ref), custom_call_target="tpu_custom_call" | custom-call | tf_op jit(solution)/shard_map/rows/pallas_call | solution.py:264
  81.6 0.6 while.64
Async XLA Ops:
  67.1 12.4 %all-to-all-start.8 = ((f32[32,1,128]{2,1,0:T(1,128)}), f32[32,1,128]{2,1,0:T(1,128)S(1)}, u32[]{:S(2)}, u32[]{:S(2)}) async-start(f32[32,1,128]{2,1,0:T(1,128)} %relay.3), calls=%async_computation.8 | async-start | bytes 32768 | tf_op jit(solution)/shard_map/all_to_all | solution.py:281

commit v9 on v7

--- a/solution.py
+++ b/solution.py
@@ -20,9 +20,9 @@
 F32 = jnp.float32
 BF16 = jnp.bfloat16
 
-FIRST = (Y,)
-FIRST_CAP = 24
-SECOND = (X, ZH)
+FIRST = (X,)
+FIRST_CAP = 32
+SECOND = (Y, ZH)
 SECOND_CAP = 16
 FAR = 4096.0
 NORM_1 = (ZH, ZL, CORE)

time: 81.4 us -> 87.1 us (1.070)
  blocking collectives: 76.1 us -> 81 us
    all_to_all x1, blocking collectives: 27.2 us -> 36.5 us  [send_on(): return (lax.all_to_all(sent, SECOND, 0, 0, tiled=True), over)]
    all_to_all x1, blocking collectives: 16.6 us -> 9.63 us  [send_first(): return (lax.all_to_all(sent, FIRST, 0, 0, tiled=True), over)]
    all_to_all x1, blocking collectives: 20.5 us -> 23.3 us  [norm_parts(): part = lax.all_to_all(part, NORM_1, 0, 0, tiled=True)]
where the time goes in v9:
time: 87.1 us; the launch traced here: 86.9 us
  blocking collectives  81 us (93%)
  Pallas kernels  4.74 us (5%)
  loops' own time  0.88 us (1%)
    all_to_all x1, blocking collectives, send_on(): return (lax.all_to_all(sent, SECOND, 0, 0, tiled=True), over)  36.5 us
    all_to_all x1, blocking collectives, norm_parts(): part = lax.all_to_all(part, NORM_1, 0, 0, tiled=True)  23.3 us
    all_to_all x1, blocking collectives, norm_parts(): return lax.all_to_all(part, NORM_2, 0, 0, tiled=True)  11.6 us
    all_to_all x1, blocking collectives, send_first(): return (lax.all_to_all(sent, FIRST, 0, 0, tiled=True), over)  9.63 us
    pallas_call x4, Pallas kernels, call(): pl.pallas_call(body, in_specs=[vmem] * len(held), out_shape=out_shape, na...  3.59 us

profile of v9, /device:TPU:1, one launch (start us, length us, event | category | flops | bytes accessed | tf_op | source)
XLA Modules:
  0.0 86.9 jit_solution(8788792470897933599)
XLA Ops:
  0.0 1.2 %first.3 = (bf16[128,640]{1,0:T(8,128)(2,1)S(1)}, f32[8,128]{1,0:T(8,128)S(1)}) custom-call(bf16[64,576]{1,0:T(8,128)(2,1)} %grad_hbm.1, s32[1,64]{1,0:T(1,128)} %bitcast.35), custom_call_target="tpu_custom_call" | custom-call | tf_op jit(solution)/shard_map/first/pallas_call | solution.py:285
  1.2 9.6 %all_to_all.70 = bf16[4,32,640]{2,1,0:T(8,128)(2,1)S(1)} all-to-all(bf16[4,32,640]{2,1,0:T(8,128)(2,1)S(1)} %bitcast.32), channel_id=1, replica_groups=mesh['dp_0'=8,'dp_1'=4,'dp_2'=3,'pipe_0'=4,'pipe_1'=2] {'dp_1'}, dimensions={0} | all-to-all | bytes 327680 | tf_op jit(solution)/shard_map/all_to_all | solution.py:296
  10.8 0.6 second.5
  11.4 36.5 %all_to_all.71 = bf16[24,16,640]{2,1,0:T(8,128)(2,1)S(1)} all-to-all(bf16[24,16,640]{2,1,0:T(8,128)(2,1)S(1)} %bitcast.31), channel_id=1, replica_groups=mesh['dp_0'=8,'dp_1'=4,'dp_2'=3,'pipe_0'=4,'pipe_1'=2] {'dp_0','dp_2'}, dimensions={0} | all-to-all | bytes 983040 | tf_op jit(solution)/shard_map/all_to_all | solution.py:270
  47.9 0.6 squares.3
  48.5 23.3 %all_to_all.72.parts_ref = f32[24,1,128]{2,1,0:T(1,128)S(1)} all-to-all(f32[24,1,128]{2,1,0:T(1,128)S(1)} %squares.3), channel_id=1, replica_groups=mesh['dp_0'=8,'dp_1'=4,'dp_2'=3,'pipe_0'=4,'pipe_1'=2] {'dp_2','pipe_0',..., dimensions={0} | all-to-all | bytes 24576 | tf_op jit(solution)/shard_map/all_to_all | solution.py:276
  71.9 11.6 %all_to_all.73.parts_ref = f32[32,1,128]{2,1,0:T(1,128)S(1)} all-to-all(f32[32,1,128]{2,1,0:T(1,128)S(1)} %relay.3), channel_id=1, replica_groups=mesh['dp_0'=8,'dp_1'=4,'dp_2'=3,'pipe_0'=4,'pipe_1'=2] {'dp_0','dp_1'}, dimensions={0} | all-to-all | bytes 32768 | tf_op jit(solution)/shard_map/all_to_all | solution.py:278
  83.5 2.3 %rows.3 = (f32[576,1408]{1,0:T(8,128)}, s32[1]{0:T(128)}) custom-call(bf16[384,640]{1,0:T(8,128)(2,1)S(1)} %bitcast.28, f32[32,1,128]{2,1,0:T(1,128)S(1)} %all_to_all.73.parts_ref), custom_call_target="tpu_custom_call" | custom-call | tf_op jit(solution)/shard_map/rows/pallas_call | solution.py:261
  85.8 0.9 %while.64 = (f32[576,1408]{1,0:T(8,128)}, s32[]{:T(128)}, s32[64]{0:T(128)}, bf16[64,576]{1,0:T(8,128)(2,1)}) while((f32[576,1408]{1,0:T(8,128)}, s32[]{:T(128)}, s32[64]{0:T(128)}, bf16[64,576]{1,0:T(8,128)(2,1)}) %tuple.86), condition=%region_15.16_spmd, body=%region_0.15_spmd | while | flops 117956688 | bytes 26263620 | solution.py:329
  (1 shorter events, 0.0 us)
